TPU v7x, 32 devices: a whole 2x2x4 slice. The times are simulated.
32 devices in a mesh: data: 2 (over x), expert: 16 (over z, y, core).
Axes of the slice: x: 2, y: 2, z: 4, core: 2. Of those that a mesh axis runs over, the one named last changes fastest.
Arguments:
- x_in: bfloat16 [32768, 512], P(('data', 'expert')), parts along dimension 0
- expert_idx: int32 [32768, 8], P(('data', 'expert')), parts along dimension 0
- gate_weight: float32 [32768, 8], P(('data', 'expert')), parts along dimension 0
- grad_y: bfloat16 [32768, 512], P(('data', 'expert')), parts along dimension 0
- w_in: bfloat16 [64, 512, 256], P('expert')
- w_out: bfloat16 [64, 256, 512], P('expert')
Outputs:
- output 1: bfloat16 [32768, 512], P(('data', 'expert')), parts along dimension 0
- output 2: bfloat16 [32768, 512], P(('data', 'expert')), parts along dimension 0
- output 3: float32 [32768, 8], P(('data', 'expert')), parts along dimension 0
- output 4: bfloat16 [128, 512, 256], P(('data', 'expert')), parts along dimension 0
- output 5: bfloat16 [128, 256, 512], P(('data', 'expert')), parts along dimension 0
There are 2 independent parts. A program takes and returns all parts, laid end to end along the dimension named above; an argument that names none is the same for every part.
All inputs are finite; a program needn't handle non-finite values.
Results may differ from a plain program's by a relative error of at most 0.0100954.
Values are sent between devices in bfloat16 or wider.
A program may use at most 1 GiB of HBM per device.

v0:
```python
import jax
import jax.numpy as jnp
from jax import lax
from jax.sharding import PartitionSpec as P

CAP_NUM = 5
CAP_DEN = 4
PAIR_FACTOR = 2


def local_ranks(flat_idx, num_experts):
    one_hot = (flat_idx[:, None] == jnp.arange(num_experts, dtype=jnp.int32)[None, :]).astype(jnp.int32)
    running = jnp.cumsum(one_hot, axis=0)
    return jnp.sum((running - one_hot) * one_hot, axis=1), running[-1]


def exchange_maps(flat_idx, local_rank, counts_all, my_index, local_experts, capacity, pair_cap):
    groups, num_experts = counts_all.shape
    n_pairs = flat_idx.shape[0]
    through = jnp.cumsum(counts_all, axis=0)
    before = through - counts_all
    kept_all = jnp.clip(capacity - before, 0, counts_all)
    before_mine = lax.dynamic_index_in_dim(before, my_index, 0, keepdims=False)
    kept_grid = lax.dynamic_index_in_dim(kept_all, my_index, 0, keepdims=False).reshape(groups, local_experts)
    send_start = (jnp.cumsum(kept_grid, axis=1) - kept_grid).reshape(num_experts)
    pair_slot = before_mine[flat_idx] + local_rank
    target = jnp.where(pair_slot < capacity, (flat_idx // local_experts) * pair_cap + send_start[flat_idx] + local_rank, groups * pair_cap)
    send_src = jnp.full((groups * pair_cap,), n_pairs, jnp.int32).at[target].set(jnp.arange(n_pairs, dtype=jnp.int32), mode='drop')
    first_expert = my_index * local_experts
    through_own = lax.dynamic_slice_in_dim(through, first_expert, local_experts, axis=1)
    before_own = lax.dynamic_slice_in_dim(before, first_expert, local_experts, axis=1)
    kept_own = lax.dynamic_slice_in_dim(kept_all, first_expert, local_experts, axis=1)
    start_own = jnp.cumsum(kept_own, axis=1) - kept_own
    slot_ids = jnp.arange(capacity, dtype=jnp.int32)
    source_dev = jnp.sum((through_own.T[:, None, :] <= slot_ids[None, :, None]).astype(jnp.int32), axis=2)
    filled = slot_ids[None, :] < jnp.minimum(through_own[-1], capacity)[:, None]
    source_dev = jnp.minimum(source_dev, groups - 1)
    start_at = jnp.take_along_axis(start_own.T, source_dev, axis=1)
    before_at = jnp.take_along_axis(before_own.T, source_dev, axis=1)
    recv_pos = jnp.where(filled, source_dev * pair_cap + start_at + slot_ids[None, :] - before_at, groups * pair_cap).reshape(local_experts * capacity)
    back_src = jnp.full((groups * pair_cap,), local_experts * capacity, jnp.int32).at[recv_pos].set(jnp.arange(local_experts * capacity, dtype=jnp.int32), mode='drop')
    return target, send_src, recv_pos, back_src


def exchange(rows):
    return lax.all_to_all(rows, 'expert', 0, 0, tiled=True)


def gather_rows(table, positions):
    return jnp.take(table, positions, axis=0, mode='fill', fill_value=0)


def solution(mesh):
    groups = mesh.shape['expert']
    tok_spec = P(('data', 'expert'), None)
    weight_spec = P('expert', None, None)
    grad_spec = P(('data', 'expert'), None, None)

    def device_pass(x_in, expert_idx, gate_weight, grad_y, w_in, w_out):
        n_tokens, top_k = expert_idx.shape
        local_experts, d_model = w_in.shape[0], w_in.shape[1]
        num_experts = local_experts * groups
        n_pairs = n_tokens * top_k
        capacity = (CAP_NUM * n_pairs * groups) // (CAP_DEN * num_experts)
        pair_cap = PAIR_FACTOR * n_pairs // groups
        my_index = lax.axis_index('expert')
        flat_idx = expert_idx.reshape(n_pairs)
        local_rank, counts = local_ranks(flat_idx, num_experts)
        counts_all = lax.all_gather(counts, 'expert')
        target, send_src, recv_pos, back_src = exchange_maps(flat_idx, local_rank, counts_all, my_index, local_experts, capacity, pair_cap)
        exp_rows = gather_rows(exchange(gather_rows(x_in, send_src // top_k)), recv_pos).reshape(local_experts, capacity, d_model)
        pre_act = jnp.einsum('lcd,ldf->lcf', exp_rows, w_in, preferred_element_type=jnp.float32)
        act_full, gelu_pull = jax.vjp(jax.nn.gelu, pre_act)
        act_bf = act_full.astype(jnp.bfloat16)
        out_rows = jnp.einsum('lcf,lfd->lcd', act_bf, w_out, preferred_element_type=jnp.float32).astype(jnp.bfloat16)
        back_out = gather_rows(out_rows.reshape(local_experts * capacity, d_model), back_src)
        out_pair = gather_rows(exchange(back_out), target).reshape(n_tokens, top_k, d_model)
        y_out = (x_in.astype(jnp.float32) + jnp.sum(gate_weight[:, :, None] * out_pair, axis=1)).astype(jnp.bfloat16)
        grad_gate = jnp.einsum('tkd,td->tk', out_pair, grad_y, preferred_element_type=jnp.float32)
        scaled_grad = (gate_weight[:, :, None] * grad_y[:, None, :]).astype(jnp.bfloat16).reshape(n_pairs, d_model)
        grad_rows = gather_rows(exchange(gather_rows(scaled_grad, send_src)), recv_pos).reshape(local_experts, capacity, d_model)
        grad_act = jnp.einsum('lcd,lfd->lcf', grad_rows, w_out, preferred_element_type=jnp.float32).astype(jnp.bfloat16)
        grad_pre = gelu_pull(grad_act.astype(jnp.float32))[0].astype(jnp.bfloat16)
        grad_w_out = jnp.einsum('lcf,lcd->lfd', act_bf, grad_rows, preferred_element_type=jnp.float32).astype(jnp.bfloat16)
        grad_w_in = jnp.einsum('lcd,lcf->ldf', exp_rows, grad_pre, preferred_element_type=jnp.float32).astype(jnp.bfloat16)
        grad_in_rows = jnp.einsum('lcf,ldf->lcd', grad_pre, w_in, preferred_element_type=jnp.float32).astype(jnp.bfloat16)
        back_grad = gather_rows(grad_in_rows.reshape(local_experts * capacity, d_model), back_src)
        grad_pair = gather_rows(exchange(back_grad), target).reshape(n_tokens, top_k, d_model)
        grad_x = (grad_y.astype(jnp.float32) + jnp.sum(grad_pair, axis=1, dtype=jnp.float32)).astype(jnp.bfloat16)
        return y_out, grad_x, grad_gate, grad_w_in, grad_w_out

    return jax.shard_map(device_pass, mesh=mesh,
                         in_specs=(tok_spec, tok_spec, tok_spec, tok_spec, weight_spec, weight_spec),
                         out_specs=(tok_spec, tok_spec, tok_spec, grad_spec, grad_spec), check_vma=False)
```

profile of v0, /device:TPU:15, one launch (start us, length us, event | category | flops | bytes accessed | tf_op | source)
XLA Modules:
  0.0 2096.0 jit_solution(8965074527272945532)
XLA Ops:
  0.7 1.0 copy.37
  2.5 1.6 fusion.14
  4.1 34.0 %reduce-window.6 = s32[64,64,128]{2,1,0:T(8,128)S(1)} reduce-window(s32[64,64,128]{2,1,0:T(8,128)} %fusion.14, s32[]{:T(128)} %constant.92.clone.1), window={size=1x1x128 pad=0_0x0_0x127_0}, to_apply=%region_0.0 | reduce-window | flops 66584576 | bytes 4194308 | tf_op jit(solution)/shard_map/reduce-window
  38.1 1.7 slice_reduce_fusion
  40.0 1.7 broadcast_add_fusion
  41.7 3.9 copy.49
  46.3 16.2 all-gather
  68.7 4.4 select_reduce_fusion
  73.1 4.4 compare_select_fusion.12
  77.6 5.8 compare_reduce_fusion.56
  83.4 4.4 compare_select_fusion.13
  87.8 72.6 %compare_and_fusion.4 = (pred[8192]{0:T(1024)(128)(4,1)}, s32[8192]{0:T(1024)}, s32[8192]{0:T(1024)S(1)}, s32[8192]{0:T(1024)S(1)}) fusion(s32[8192]{0:T(1024)S(1)} %select_reduce_fusion, s32[8192]{0:T(1024)S(1)} %eq.29, pred[8192]{0:T(1024)(128)(4,1)S(1)} %get-tuple-element.65, pred[8192]{0:T(1024)(128)(4,1)S(1)} %get-tuple-element.64, ...), kind=kLoop, calls=%fused_computation.178 | loop fusion | flops 1155072 | bytes 704968 | tf_op jit(solution)/shard_map/jit(_take)/and | solution.py:50
  160.6 30.7 %scatter_custom_fusion = s32[16384]{0:T(1024)S(1)} fusion(s32[8192]{0:T(1024)S(1)} %bitcast.224, s32[8192]{0:T(1024)S(1)} %iota.21, s32[]{:T(128)} %constant.85.clone.1), kind=kCustom, calls=%fused_computation.175 | custom fusion | bytes 65540 | tf_op jit(solution)/shard_map/scatter | solution.py:28
  192.3 4.0 fusion
  196.3 71.0 %gather_fusion.1 = bf16[16384,512]{1,0:T(8,128)(2,1)} fusion(bf16[8192,512]{1,0:T(8,128)(2,1)} %fusion, s32[16384]{0:T(1024)S(1)} %get-tuple-element.78), kind=kCustom, calls=%fused_computation.9 | custom fusion | bytes 33619968 | tf_op jit(solution)/shard_map/jit(_take)/gather | solution.py:50
  267.3 14.4 broadcast_select_fusion.2
  281.7 11.7 all-to-all-start.2
  293.5 66.1 %gather_fusion = bf16[16384,512]{1,0:T(8,128)(2,1)} fusion(bf16[1024,512]{1,0:T(8,128)(2,1)S(1)} %copy-done.2, s32[16384]{0:T(1024)S(1)} %get-tuple-element.79), kind=kCustom, calls=%fused_computation.8 | custom fusion | bytes 33619968 | tf_op jit(solution)/shard_map/jit(_take)/gather | solution.py:50
  359.6 14.4 broadcast_select_fusion.3
  374.0 281.9 %all-to-all-done.2 = bf16[16,1024,512]{2,1,0:T(8,128)(2,1)} async-done(((bf16[16,1024,512]{2,1,0:T(8,128)(2,1)}), bf16[16,1024,512]{2,1,0:T(8,128)(2,1)}, u32[]{:S(2)}, u32[]{:S(2)}) %all-to-all-start.2) | async-done | bytes 16777248 | tf_op jit(solution)/shard_map/all_to_all | solution.py:46
  656.0 5.0 all-to-all-start
  661.7 68.2 %gather_fusion.3 = s32[10240]{0:T(1024)S(1)} fusion(s32[4,16]{0,1:T(8,128)S(1)} %get-tuple-element.212, s32[10240]{0:T(1024)S(1)} %reshape.840), kind=kCustom, calls=%fused_computation.4.clone | custom fusion | bytes 163840 | tf_op jit(solution)/shard_map/jit(take_along_axis)/gather | solution.py:39
  729.9 68.2 %gather_fusion.2 = s32[10240]{0:T(1024)S(1)} fusion(s32[4,16]{0,1:T(8,128)S(1)} %subtract_bitcast_fusion, s32[10240]{0:T(1024)S(1)} %reshape.840), kind=kCustom, calls=%fused_computation.clone | custom fusion | bytes 163840 | tf_op jit(solution)/shard_map/jit(take_along_axis)/gather | solution.py:38
  798.5 37.9 %scatter_custom_fusion.1 = s32[16384]{0:T(1024)S(1)} fusion(s32[10240]{0:T(1024)S(1)} %bitcast.222, s32[10240]{0:T(1024)S(1)} %iota.22, s32[]{:T(128)} %constant.150.clone.1), kind=kCustom, calls=%fused_computation.173 | custom fusion | bytes 65540 | tf_op jit(solution)/shard_map/scatter | solution.py:41
  837.1 50.3 %gather_fusion.7 = bf16[10240,512]{1,0:T(8,128)(2,1)} fusion(bf16[16384,512]{1,0:T(8,128)(2,1)} %bitcast.156, s32[10240]{0:T(1024)S(1)} %fusion.21), kind=kCustom, calls=%fused_computation.5.clone | custom fusion | bytes 21012480 | tf_op jit(solution)/shard_map/jit(_take)/gather | solution.py:50
  887.4 135.7 %all-to-all-done = bf16[16,1024,512]{2,1,0:T(8,128)(2,1)} async-done(((bf16[16,1024,512]{2,1,0:T(8,128)(2,1)}), bf16[16,1024,512]{2,1,0:T(8,128)(2,1)}, u32[]{:S(2)}, u32[]{:S(2)}) %all-to-all-start) | async-done | bytes 16777248 | tf_op jit(solution)/shard_map/all_to_all | solution.py:46
  1023.1 49.9 %gather_fusion.4 = bf16[10240,512]{1,0:T(8,128)(2,1)} fusion(bf16[16384,512]{1,0:T(8,128)(2,1)} %bitcast.148, s32[10240]{0:T(1024)S(1)} %fusion.21), kind=kCustom, calls=%fused_computation.1.clone | custom fusion | bytes 21012480 | tf_op jit(solution)/shard_map/jit(_take)/gather | solution.py:50
  1073.0 12.7 broadcast_select_fusion.4
  1085.6 6.0 fusion.43
  1091.7 1.0 copy-done.4
  1092.6 8.8 convolution_convert_fusion.1
  1101.4 13.0 fusion.3
  1114.5 5.7 convolution_convert_fusion
  1120.2 71.9 %gather_fusion.8 = bf16[16384,512]{1,0:T(8,128)(2,1)} fusion(bf16[10240,512]{1,0:T(8,128)(2,1)} %bitcast.199, s32[16384]{0:T(1024)S(1)} %fusion.18), kind=kCustom, calls=%fused_computation.6.clone | custom fusion | bytes 33619968 | tf_op jit(solution)/shard_map/jit(_take)/gather | solution.py:50
  1192.1 71.9 %gather_fusion.5 = bf16[16384,512]{1,0:T(8,128)(2,1)} fusion(bf16[10240,512]{1,0:T(8,128)(2,1)} %bitcast.200, s32[16384]{0:T(1024)S(1)} %fusion.18), kind=kCustom, calls=%fused_computation.2.clone | custom fusion | bytes 33619968 | tf_op jit(solution)/shard_map/jit(_take)/gather | solution.py:50
  1264.0 22.8 %broadcast_select_fusion.1 = (bf16[16384,512]{1,0:T(8,128)(2,1)}, bf16[16384,512]{1,0:T(8,128)(2,1)}) fusion(bf16[16384,512]{1,0:T(8,128)(2,1)} %gather_fusion.5, pred[16384]{0:T(1024)(128)(4,1)S(1)} %copy-done.13, bf16[16384,512]{1,0:T(8,128)(2,1)} %gather_fusion.8), kind=kLoop, calls=%fused_computation.17 | loop fusion | flops 16777216 | bytes 67125248 | tf_op jit(solution)/shard_map/jit(_take)/select_n | solution.py:50
  1286.8 367.6 %all_to_all.42 = bf16[16,1024,512]{2,1,0:T(8,128)(2,1)} all-to-all(bf16[16,1024,512]{2,1,0:T(8,128)(2,1)} %bitcast.203), channel_id=1, replica_groups=mesh['data'=2,'expert'=16] {'expert'}, dimensions={0} | all-to-all | bytes 33554432 | tf_op jit(solution)/shard_map/all_to_all | solution.py:46
  1654.3 5.6 all-to-all-start.1
  1659.9 10.0 convolution_convert_fusion.4
  1670.0 11.2 convolution_convert_fusion.3
  1681.2 41.7 %gather_fusion.9 = bf16[8192,512]{1,0:T(8,128)(2,1)} fusion(bf16[16384,512]{1,0:T(8,128)(2,1)} %bitcast.201, s32[8192]{0:T(1024)S(1)} %broadcast_clamp_fusion.1), kind=kCustom, calls=%fused_computation.7.clone | custom fusion | bytes 16809984 | tf_op jit(solution)/shard_map/jit(_take)/gather | solution.py:50
  1722.9 299.5 %all-to-all-done.1 = bf16[16,1024,512]{2,1,0:T(8,128)(2,1)} async-done(((bf16[16,1024,512]{2,1,0:T(8,128)(2,1)}), bf16[16,1024,512]{2,1,0:T(8,128)(2,1)}, u32[]{:S(2)}, u32[]{:S(2)}) %all-to-all-start.1) | async-done | bytes 16777248 | tf_op jit(solution)/shard_map/all_to_all | solution.py:46
  2022.4 41.8 %gather_fusion.6 = bf16[8192,512]{1,0:T(8,128)(2,1)} fusion(bf16[16384,512]{1,0:T(8,128)(2,1)} %bitcast.152, s32[8192]{0:T(1024)S(1)} %broadcast_clamp_fusion.1), kind=kCustom, calls=%fused_computation.3.clone | custom fusion | bytes 16809984 | tf_op jit(solution)/shard_map/jit(_take)/gather | solution.py:50
  2064.2 16.2 convert_reduce_fusion
  2080.4 7.8 fusion.11
  2088.2 1.8 copy.46
  2089.9 2.9 add_convert_fusion
  2092.8 2.9 add_convert_fusion.1
  (81 shorter events, 10.7 us)
Async XLA Ops:
  0.6 1092.0 %copy-start = (bf16[4,256,512]{2,1,0:T(8,128)(2,1)S(1)}, bf16[4,256,512]{2,1,0:T(8,128)(2,1)}, u32[]{:S(2)}) copy-start(bf16[4,256,512]{2,1,0:T(8,128)(2,1)} %param.19) | copy-start | bytes 3145732
  38.1 153.4 %copy-start.15 = (f32[1024,8]{0,1:T(8,128)S(1)}, f32[1024,8]{0,1:T(8,128)}, u32[]{:S(2)}) copy-start(f32[1024,8]{0,1:T(8,128)} %param.16) | copy-start | bytes 98308
  41.7 150.2 %copy-start.10 = (bf16[1024,512]{1,0:T(8,128)(2,1)S(1)}, bf16[1024,512]{1,0:T(8,128)(2,1)}, u32[]{:S(2)}) copy-start(bf16[1024,512]{1,0:T(8,128)(2,1)} %param.17) | copy-start | bytes 3145732
  191.7 75.6 %copy-start.8 = (f32[1024,8]{1,0:T(8,128)}, f32[1024,8]{1,0:T(8,128)S(1)}, u32[]{:S(2)}) copy-start(f32[1024,8]{1,0:T(8,128)S(1)} %copy.36) | copy-start | bytes 98308
  281.7 11.8 copy-start.2
  281.7 374.3 %all-to-all-start.2 = ((bf16[16,1024,512]{2,1,0:T(8,128)(2,1)}), bf16[16,1024,512]{2,1,0:T(8,128)(2,1)}, u32[]{:S(2)}, u32[]{:S(2)}) async-start(bf16[16,1024,512]{2,1,0:T(8,128)(2,1)} %broadcast_select_fusion.2), calls=%async_computation.2 | async-start | bytes 33554432 | tf_op jit(solution)/shard_map/all_to_all | solution.py:46
  656.0 367.1 %all-to-all-start = ((bf16[16,1024,512]{2,1,0:T(8,128)(2,1)}), bf16[16,1024,512]{2,1,0:T(8,128)(2,1)}, u32[]{:S(2)}, u32[]{:S(2)}) async-start(bf16[16,1024,512]{2,1,0:T(8,128)(2,1)} %broadcast_select_fusion.3), calls=%async_computation | async-start | bytes 33554432 | tf_op jit(solution)/shard_map/all_to_all | solution.py:46
  1073.0 12.7 copy-start.7
  1085.6 7.0 copy-start.4
  1114.5 5.8 copy-start.6
  1192.1 71.9 %copy-start.13 = (pred[16384]{0:T(1024)(128)(4,1)S(1)}, pred[16384]{0:T(1024)(128)(4,1)}, u32[]{:S(2)}) copy-start(pred[16384]{0:T(1024)(128)(4,1)} %compare_and_fusion) | copy-start | bytes 49156
  1654.3 5.6 copy-start.12
  1654.3 368.1 %all-to-all-start.1 = ((bf16[16,1024,512]{2,1,0:T(8,128)(2,1)}), bf16[16,1024,512]{2,1,0:T(8,128)(2,1)}, u32[]{:S(2)}, u32[]{:S(2)}) async-start(bf16[16,1024,512]{2,1,0:T(8,128)(2,1)} %bitcast.202), calls=%async_computation.1 | async-start | bytes 33554432 | tf_op jit(solution)/shard_map/all_to_all | solution.py:46
  2022.4 41.8 %copy-start.9 = (f32[1024,8]{1,0:T(8,128)S(1)}, f32[1024,8]{1,0:T(8,128)}, u32[]{:S(2)}) copy-start(f32[1024,8]{1,0:T(8,128)} %copy-done.8) | copy-start | bytes 98308
  2022.4 41.8 %copy-start.14 = (pred[8192]{0:T(1024)(128)(4,1)S(1)}, pred[8192]{0:T(1024)(128)(4,1)}, u32[]{:S(2)}) copy-start(pred[8192]{0:T(1024)(128)(4,1)} %get-tuple-element.68) | copy-start | bytes 24580
  2064.2 16.2 copy-start.5
  2064.2 16.2 copy-start.11
  2080.4 12.5 copy-start.3
  2080.4 15.4 copy-start.1
where the time goes:
time: 2100 us
  waiting for transfers between devices  717 us (34%)
  local copies, waits for them, and re-layouts  687 us (33%)
  blocking collectives  384 us (18%)
  other arithmetic  222 us (11%)
  matrix products  62.7 us (3%)
  starting transfers between devices  22.3 us (1%)
    all_to_all x3, waiting for transfers between devices, exchange(): return lax.all_to_all(rows, 'expert', 0, 0, tiled=True)  717 us
    gather x8, local copies, waits for them, and re-layouts, gather_rows(): return jnp.take(table, positions, axis=0, mode='fill', fill_value=0)  464 us
    all_to_all x1, blocking collectives, exchange(): return lax.all_to_all(rows, 'expert', 0, 0, tiled=True)  368 us
    and x4, other arithmetic, gather_rows(): return jnp.take(table, positions, axis=0, mode='fill', fill_value=0)  73.3 us
    gather x3, local copies, waits for them, and re-layouts, exchange_maps(): start_at = jnp.take_along_axis(start_own.T, source_dev, axis=1)  68.2 us
    gather x2, local copies, waits for them, and re-layouts, exchange_maps(): before_at = jnp.take_along_axis(before_own.T, source_dev, axis=1)  68.2 us
    select_n x4, other arithmetic, gather_rows(): return jnp.take(table, positions, axis=0, mode='fill', fill_value=0)  64.4 us
  transfers between devices with their start and end apart: 3, of which 3 were waited for; matrix products, arithmetic and copies ran while one was open for 18% of the time, Pallas kernels for 0%

commit v1 on v0

v1 whole, which is shorter than its diff:
```python
import functools

import jax
import jax.numpy as jnp
from jax import lax
from jax.experimental import pallas as pl
from jax.experimental.pallas import tpu as pltpu
from jax.sharding import PartitionSpec as P

CAP_NUM = 5
CAP_DEN = 4
PAIR_FACTOR = 2

TILE = 128
ALIGN = 8
LANES = 128
TOKENS_PER_STEP = 16
VMEM_BYTES = 62 * 1024 * 1024
GELU_C = 0.7978845608028654
GELU_K = 0.044715


def ceil_to(n, m):
    return (n + m - 1) // m * m


def gelu_parts(a):
    sq = a * a
    t = jnp.tanh(GELU_C * (a + GELU_K * (sq * a)))
    cdf = 0.5 * (1.0 + t)
    slope = cdf + (0.5 * a) * (1.0 - t * t) * (GELU_C * (1.0 + (3.0 * GELU_K) * sq))
    return a * cdf, slope


def dot_nn(a, b):
    return jnp.dot(a, b, preferred_element_type=jnp.float32)


def dot_nt(a, b):
    return lax.dot_general(a, b, (((1,), (1,)), ((), ())), preferred_element_type=jnp.float32)


def dot_tn(a, b):
    return lax.dot_general(a, b, (((0,), (0,)), ((), ())), preferred_element_type=jnp.float32)


def pick_matrix(meta, n_tokens):
    tok = meta[:, 0:1].astype(jnp.int32)
    cols = lax.broadcasted_iota(jnp.int32, (meta.shape[0], n_tokens), 1)
    return jnp.where(tok == cols, 1.0, 0.0).astype(jnp.bfloat16)


def token_kernel(zero_row, top_k, sc_ref, pos_ref, meta_ref, x_ref, dy_ref, w1_ref, w2_ref,
                 y_ref, dx_ref, dg_ref, buf, dgb, tmp, tmpg):
    e = pl.program_id(0)
    n_tokens, d = x_ref.shape

    @pl.when(e == 0)
    def _():
        buf[pl.ds(zero_row, ALIGN), :] = jnp.zeros((ALIGN, 2 * d), jnp.float32)
        dgb[pl.ds(zero_row, ALIGN), :] = jnp.zeros((ALIGN, LANES), jnp.float32)

    list_start, buf_start, kept = sc_ref[0, e], sc_ref[1, e], sc_ref[2, e]

    def tile(i, carry):
        meta = meta_ref[pl.ds(pl.multiple_of(list_start + i * TILE, ALIGN), TILE), :]
        pick = pick_matrix(meta, n_tokens)
        gate = meta[:, 1:2]
        rows = dot_nn(pick, x_ref[...]).astype(jnp.bfloat16)
        drow = dot_nn(pick, dy_ref[...])
        act, slope = gelu_parts(dot_nn(rows, w1_ref[0]))
        out = dot_nn(act.astype(jnp.bfloat16), w2_ref[0]).astype(jnp.bfloat16).astype(jnp.float32)
        grad = (gate * drow).astype(jnp.bfloat16)
        dact = dot_nt(grad, w2_ref[0]).astype(jnp.bfloat16).astype(jnp.float32)
        dpre = (dact * slope).astype(jnp.bfloat16)
        din = dot_nt(dpre, w1_ref[0]).astype(jnp.bfloat16).astype(jnp.float32)
        at = pl.ds(pl.multiple_of(buf_start + i * TILE, ALIGN), TILE)
        buf[at, 0:d] = gate * out
        buf[at, d:2 * d] = din
        dgb[at, :] = jnp.broadcast_to(jnp.sum(drow * out, axis=1, keepdims=True), (TILE, LANES))
        return carry

    lax.fori_loop(0, (kept + TILE - 1) // TILE, tile, 0)

    @pl.when(e == pl.num_programs(0) - 1)
    def _():
        lane = lax.broadcasted_iota(jnp.int32, (1, LANES), 1)

        def block(b, carry):
            for k in range(TOKENS_PER_STEP):
                acc, dg = None, jnp.zeros((1, LANES), jnp.float32)
                for j in range(top_k):
                    r = pos_ref[(b * TOKENS_PER_STEP + k) * top_k + j]
                    row = buf[pl.ds(r, 1), :]
                    acc = row if acc is None else acc + row
                    dg = jnp.where(lane == j, dgb[pl.ds(r, 1), :], dg)
                tmp[k:k + 1, :] = acc
                tmpg[k:k + 1, :] = dg
            at = pl.ds(pl.multiple_of(b * TOKENS_PER_STEP, TOKENS_PER_STEP), TOKENS_PER_STEP)
            y_ref[at, :] = (x_ref[at, :].astype(jnp.float32) + tmp[:, 0:d]).astype(jnp.bfloat16)
            dx_ref[at, :] = (dy_ref[at, :].astype(jnp.float32) + tmp[:, d:2 * d]).astype(jnp.bfloat16)
            dg_ref[at, :] = tmpg[...]
            return carry

        lax.fori_loop(0, n_tokens // TOKENS_PER_STEP, block, 0)


def token_pass(scalars, pos, meta, block_rows, x, dy, w1, w2, buf_rows, zero_row, top_k):
    n_tokens, d = x.shape
    experts, _, f = w1.shape
    per_dev = experts * block_rows // meta.shape[0]
    whole = lambda e, *_: (0, 0)
    return pl.pallas_call(
        functools.partial(token_kernel, zero_row, top_k),
        out_shape=(jax.ShapeDtypeStruct((n_tokens, d), jnp.bfloat16),
                   jax.ShapeDtypeStruct((n_tokens, d), jnp.bfloat16),
                   jax.ShapeDtypeStruct((n_tokens, LANES), jnp.float32)),
        grid_spec=pltpu.PrefetchScalarGridSpec(
            num_scalar_prefetch=2, grid=(experts,),
            in_specs=[pl.BlockSpec((block_rows, 2), lambda e, *_: (e // per_dev, 0)),
                      pl.BlockSpec((n_tokens, d), whole, pipeline_mode=pl.Buffered(1)),
                      pl.BlockSpec((n_tokens, d), whole, pipeline_mode=pl.Buffered(1)),
                      pl.BlockSpec((1, d, f), lambda e, *_: (e, 0, 0)),
                      pl.BlockSpec((1, f, d), lambda e, *_: (e, 0, 0))],
            out_specs=[pl.BlockSpec((n_tokens, d), whole, pipeline_mode=pl.Buffered(1)),
                       pl.BlockSpec((n_tokens, d), whole, pipeline_mode=pl.Buffered(1)),
                       pl.BlockSpec((n_tokens, LANES), whole, pipeline_mode=pl.Buffered(1))],
            scratch_shapes=[pltpu.VMEM((buf_rows, 2 * d), jnp.float32),
                            pltpu.VMEM((buf_rows, LANES), jnp.float32),
                            pltpu.VMEM((TOKENS_PER_STEP, 2 * d), jnp.float32),
                            pltpu.VMEM((TOKENS_PER_STEP, LANES), jnp.float32)]),
        compiler_params=pltpu.CompilerParams(dimension_semantics=("arbitrary",), vmem_limit_bytes=VMEM_BYTES),
        cost_estimate=pl.CostEstimate(flops=60_000_000_000, bytes_accessed=40_000_000, transcendentals=4_000_000),
        name="token_pass",
    )(scalars, pos, meta, x, dy, w1, w2)


def owner_kernel(sc_ref, meta_ref, x_ref, dy_ref, w1_ref, w2_ref, dw1_ref, dw2_ref, acc1, acc2):
    s = pl.program_id(0)
    n_tokens, d = x_ref.shape
    local_experts = w1_ref.shape[0]

    @pl.when(s == 0)
    def _():
        acc1[...] = jnp.zeros_like(acc1)
        acc2[...] = jnp.zeros_like(acc2)

    for e in range(local_experts):
        start, kept = sc_ref[0, s * local_experts + e], sc_ref[1, s * local_experts + e]

        def tile(i, carry, e=e, start=start, kept=kept):
            meta = meta_ref[pl.ds(pl.multiple_of(start + i * TILE, ALIGN), TILE), :]
            pick = pick_matrix(meta, n_tokens)
            live = lax.broadcasted_iota(jnp.int32, (TILE, 1), 0) + i * TILE < kept
            gate = jnp.where(live, meta[:, 1:2], 0.0)
            rows = dot_nn(pick, x_ref[...]).astype(jnp.bfloat16)
            grad = (gate * dot_nn(pick, dy_ref[...])).astype(jnp.bfloat16)
            act, slope = gelu_parts(dot_nn(rows, w1_ref[e]))
            dact = dot_nt(grad, w2_ref[e]).astype(jnp.bfloat16).astype(jnp.float32)
            dpre = (dact * slope).astype(jnp.bfloat16)
            acc2[e] += dot_tn(act.astype(jnp.bfloat16), grad)
            acc1[e] += dot_tn(rows, dpre)
            return carry

        lax.fori_loop(0, (kept + TILE - 1) // TILE, tile, 0)

    @pl.when(s == pl.num_programs(0) - 1)
    def _():
        dw1_ref[...] = acc1[...].astype(jnp.bfloat16)
        dw2_ref[...] = acc2[...].astype(jnp.bfloat16)


def owner_pass(scalars, meta, x_all, dy_all, w1, w2, sources):
    local_experts, d, f = w1.shape
    n_tokens = x_all.shape[0] // sources
    block_rows = meta.shape[0] // sources
    return pl.pallas_call(
        owner_kernel,
        out_shape=(jax.ShapeDtypeStruct(w1.shape, jnp.bfloat16), jax.ShapeDtypeStruct(w2.shape, jnp.bfloat16)),
        grid_spec=pltpu.PrefetchScalarGridSpec(
            num_scalar_prefetch=1, grid=(sources,),
            in_specs=[pl.BlockSpec((block_rows, 2), lambda s, *_: (s, 0)),
                      pl.BlockSpec((n_tokens, d), lambda s, *_: (s, 0)),
                      pl.BlockSpec((n_tokens, d), lambda s, *_: (s, 0)),
                      pl.BlockSpec(w1.shape, lambda s, *_: (0, 0, 0)),
                      pl.BlockSpec(w2.shape, lambda s, *_: (0, 0, 0))],
            out_specs=[pl.BlockSpec(w1.shape, lambda s, *_: (0, 0, 0)),
                       pl.BlockSpec(w2.shape, lambda s, *_: (0, 0, 0))],
            scratch_shapes=[pltpu.VMEM(w1.shape, jnp.float32), pltpu.VMEM(w2.shape, jnp.float32)]),
        compiler_params=pltpu.CompilerParams(dimension_semantics=("arbitrary",), vmem_limit_bytes=VMEM_BYTES // 2),
        cost_estimate=pl.CostEstimate(flops=50_000_000_000, bytes_accessed=50_000_000, transcendentals=3_000_000),
        name="owner_pass",
    )(scalars, meta, x_all, dy_all, w1, w2)


def split3(v):
    a = lax.reduce_precision(v, 8, 7)
    b = lax.reduce_precision(v - a, 8, 7)
    return a, b, lax.reduce_precision(v - a - b, 8, 7)


def route(expert_idx, gate, num_experts, groups, list_rows):
    n_tokens, top_k = expert_idx.shape
    n_pairs = n_tokens * top_k
    local_experts = num_experts // groups
    chunk = 256
    flat = expert_idx.reshape(n_pairs)
    hot = (flat[:, None] == jnp.arange(num_experts, dtype=jnp.int32)[None, :])
    hot_b = hot.astype(jnp.bfloat16).reshape(n_pairs // chunk, chunk, num_experts)
    lower = jnp.tril(jnp.ones((chunk, chunk), jnp.bfloat16), -1)
    inner = jnp.einsum('ij,bje->bie', lower, hot_b, preferred_element_type=jnp.float32)
    sums = jnp.sum(hot_b.astype(jnp.float32), axis=1)
    through = jnp.cumsum(sums, axis=0)
    ranks = inner + (through - sums)[:, None, :]
    counts = through[-1].astype(jnp.int32)
    padded = (counts + ALIGN - 1) // ALIGN * ALIGN
    grid = padded.reshape(groups, local_experts)
    local_start = (jnp.cumsum(grid, axis=1) - grid).reshape(num_experts)
    list_start = local_start + jnp.repeat(jnp.arange(groups, dtype=jnp.int32) * list_rows, local_experts)
    rank = jnp.sum(hot_b.astype(jnp.float32) * ranks, axis=2).reshape(n_pairs).astype(jnp.int32)
    start_of = jnp.sum(jnp.where(hot, list_start[None, :], 0), axis=1)
    list_pos = start_of + rank
    hi = (list_pos[:, None] // LANES == jnp.arange(groups * list_rows // LANES, dtype=jnp.int32)[None, :]).astype(jnp.bfloat16)
    lo = list_pos[:, None] % LANES == jnp.arange(LANES, dtype=jnp.int32)[None, :]
    token = jnp.arange(n_pairs, dtype=jnp.int32) // top_k
    parts = [(token // 32).astype(jnp.float32), (token % 32).astype(jnp.float32), *split3(gate.reshape(n_pairs))]
    vals = jnp.concatenate([jnp.where(lo, v[:, None], 0.0).astype(jnp.bfloat16) for v in parts], axis=1)
    lists = lax.dot_general(hi, vals, (((0,), (0,)), ((), ())), preferred_element_type=jnp.float32)
    t_hi, t_lo, g1, g2, g3 = (lists[:, k * LANES:(k + 1) * LANES] for k in range(5))
    return flat, hot, rank, counts, padded, local_start, 32.0 * t_hi + t_lo, g1 + g2 + g3


def columns(tokens, gates):
    return jnp.stack([tokens.reshape(-1), gates.reshape(-1)], axis=1)


def solution(mesh):
    groups = mesh.shape['expert']
    tok_spec = P(('data', 'expert'), None)
    weight_spec = P('expert', None, None)
    grad_spec = P(('data', 'expert'), None, None)

    def device_pass(x_in, expert_idx, gate_weight, grad_y, w_in, w_out):
        n_tokens, top_k = expert_idx.shape
        local_experts = w_in.shape[0]
        num_experts = local_experts * groups
        n_pairs = n_tokens * top_k
        capacity = (CAP_NUM * n_pairs * groups) // (CAP_DEN * num_experts)
        pair_cap = PAIR_FACTOR * n_pairs // groups
        list_rows = ceil_to(pair_cap + local_experts * (ALIGN - 1) + TILE, LANES)
        me = lax.axis_index('expert')

        w1_all = lax.all_gather(w_in, 'expert', axis=0, tiled=True)
        w2_all = lax.all_gather(w_out, 'expert', axis=0, tiled=True)

        flat, hot, rank, counts, padded, local_start, tok_list, gate_list = route(
            expert_idx, gate_weight, num_experts, groups, list_rows)
        counts_all = lax.all_gather(counts, 'expert')
        before = jnp.cumsum(counts_all, axis=0) - counts_all
        kept_all = jnp.clip(capacity - before, 0, counts_all)
        kept_mine = lax.dynamic_index_in_dim(kept_all, me, 0, keepdims=False)

        buf_start = jnp.cumsum(padded) - padded
        zero_row = n_pairs + num_experts * (ALIGN - 1) + TILE
        buf_rows = zero_row + ALIGN
        pick = lambda v: jnp.sum(jnp.where(hot, v[None, :], 0), axis=1)
        pos = jnp.where(rank < pick(kept_mine), pick(buf_start) + rank, zero_row)
        token_scalars = jnp.stack([local_start, buf_start, kept_mine])
        y_out, grad_x, grad_gate = token_pass(token_scalars, pos, columns(tok_list, gate_list), list_rows,
                                              x_in, grad_y, w1_all, w2_all, buf_rows, zero_row, top_k)

        grid_all = ((counts_all + ALIGN - 1) // ALIGN * ALIGN).reshape(groups, groups, local_experts)
        start_all = jnp.cumsum(grid_all, axis=2) - grid_all
        start_own = lax.dynamic_index_in_dim(start_all, me, 1, keepdims=False).reshape(-1)
        kept_own = lax.dynamic_index_in_dim(kept_all.reshape(groups, groups, local_experts), me, 1, keepdims=False).reshape(-1)
        lists = jnp.stack([tok_list.reshape(groups, -1, LANES), gate_list.reshape(groups, -1, LANES)], axis=1)
        lists = lax.all_to_all(lists, 'expert', 0, 0, tiled=True)
        x_all = lax.all_gather(x_in, 'expert', axis=0, tiled=True)
        dy_all = lax.all_gather(grad_y, 'expert', axis=0, tiled=True)
        grad_w_in, grad_w_out = owner_pass(jnp.stack([start_own, kept_own]), columns(lists[:, 0], lists[:, 1]),
                                           x_all, dy_all, w_in, w_out, groups)
        return y_out, grad_x, grad_gate[:, :top_k], grad_w_in, grad_w_out

    return jax.shard_map(device_pass, mesh=mesh,
                         in_specs=(tok_spec, tok_spec, tok_spec, tok_spec, weight_spec, weight_spec),
                         out_specs=(tok_spec, tok_spec, tok_spec, grad_spec, grad_spec), check_vma=False)
```

time: 2100 us -> 612 us (0.29)
  local copies, waits for them, and re-layouts: 687 us -> 21.1 us
  waiting for transfers between devices: 717 us -> 339 us
  blocking collectives: 384 us -> 15.7 us
  other arithmetic: 222 us -> 20.5 us
  Pallas kernels: 0 us -> 185 us
  matrix products: 62.7 us -> 3.32 us
    all_to_all x3 -> x1, waiting for transfers between devices: 717 us -> 3.5 us  [device_pass(): lists = lax.all_to_all(lists, 'expert', 0, 0, tiled=True)]
    gather x21 -> x0, local copies, waits for them, and re-layouts: 607 us -> none  [the longest x8 464 us: gather_rows(): return jnp.take(table, positions, axis=0, mode='fill', fill_value=0)]
    all_to_all x1 -> x0, blocking collectives: 368 us -> none  [exchange(): return lax.all_to_all(rows, 'expert', 0, 0, tiled=True)]
    all_gather x0 -> x4, waiting for transfers between devices: none -> 333 us  [the longest x1 127 us: device_pass(): w2_all = lax.all_gather(w_out, 'expert', axis=0, tiled=True)]
    pallas_call x0 -> x2, Pallas kernels: none -> 185 us  [the longest x1 105 us: token_pass(): pl.pallas_call(functools.partial(token_kernel, zero_row, top_k), out_shap...]
    and x4 -> x0, other arithmetic: 73.3 us -> none  [gather_rows(): return jnp.take(table, positions, axis=0, mode='fill', fill_value=0)]
    scatter x2 -> x0, local copies, waits for them, and re-layouts: 68.6 us -> none  [the longest x1 37.9 us: exchange_maps(): jnp.full((groups * pair_cap,), local_experts * capacity, jnp.int32)]
    select_n x7 -> x1, other arithmetic: 64.7 us -> 0.65 us  [route(): list_pos[:, None] // LANES]
  transfers between devices with their start and end apart: 3 -> 5, of which waited for: 3 -> 5; matrix products, arithmetic and copies ran while one was open for 18% -> 7% of each run, Pallas kernels for 0% -> 17%
where the time goes in v1:
time: 612 us; the launch traced here: 608 us
  waiting for transfers between devices  339 us (55%)
  Pallas kernels  185 us (30%)
  local copies, waits for them, and re-layouts  21.1 us (3%)
  other arithmetic  20.5 us (3%)
  blocking collectives  15.7 us (3%)
  between operations  14.1 us (2%)
  starting transfers between devices  10.2 us (2%)
    all_gather x1, waiting for transfers between devices, device_pass(): w2_all = lax.all_gather(w_out, 'expert', axis=0, tiled=True)  127 us
    all_gather x1, waiting for transfers between devices, device_pass(): dy_all = lax.all_gather(grad_y, 'expert', axis=0, tiled=True)  126 us
    pallas_call x1, Pallas kernels, token_pass(): pl.pallas_call(functools.partial(token_kernel, zero_row, top_k), out_shap...  105 us
    pallas_call x1, Pallas kernels, owner_pass(): pl.pallas_call(owner_kernel, out_shape=(jax.ShapeDtypeStruct(w1.shape, jn...  80.4 us
    all_gather x1, waiting for transfers between devices, device_pass(): w1_all = lax.all_gather(w_in, 'expert', axis=0, tiled=True)  58.9 us
    all_gather x1, waiting for transfers between devices, device_pass(): x_all = lax.all_gather(x_in, 'expert', axis=0, tiled=True)  20.2 us
    all_gather x1, blocking collectives, device_pass(): counts_all = lax.all_gather(counts, 'expert')  15.7 us
    unnamed x6, other arithmetic  13.3 us
  transfers between devices with their start and end apart: 5, of which 5 were waited for; matrix products, arithmetic and copies ran while one was open for 7% of the time, Pallas kernels for 17%

profile of v1, /device:TPU:15, one launch (start us, length us, event | category | flops | bytes accessed | tf_op | source)
XLA Modules:
  0.0 608.4 jit_solution(1849380076603911011)
XLA Ops:
  7.2 0.7 all-gather.6.cloned.1.call-update
  8.0 0.7 all-gather.8.cloned.1.call-update
  8.7 0.7 all-gather.10.cloned.1.call-update
  9.4 0.5 all-gather.12.cloned.1.call-update
  10.0 0.2 copy.40
  10.2 0.3 eq.55
  10.5 0.2 eq.59
  10.7 0.3 convert_reduce_fusion
  11.2 15.7 %all-gather = s32[16,1,64]{2,1,0:T(1,128)S(1)} all-gather(s32[1,1,64]{2,1,0:T(1,128)S(1)} %fusion.36), channel_id=1, replica_groups=mesh['data'=2,'expert'=16] {'expert'}, dimensions={0}, use_global_device_ids=true | all-gather | bytes 4352 | tf_op jit(solution)/shard_map/all_gather | solution.py:258
  27.0 0.1 reshape.211
  27.1 0.1 sub.97
  27.2 0.2 reduce_window_sum.54
  27.4 0.1 reduce_window_sum.55
  27.5 0.2 reduce-window_clone.1
  27.7 0.9 fusion.2
  28.7 0.2 copy.42
  28.9 0.3 reshape.212
  29.2 0.8 select_reduce_fusion
  30.1 0.6 add_select_fusion.4
  30.7 2.7 fusion.3
  33.5 3.5 fusion.4
  37.0 3.5 fusion.5
  40.5 3.5 fusion.6
  44.1 3.8 fusion.7
  47.8 2.4 fusion
  50.4 0.8 copy.48
  51.2 10.0 %all-to-all-start = ((f32[16,2,10,128]{3,1,2,0:T(2,128)}), f32[16,2,10,128]{3,1,2,0:T(2,128)S(1)}, u32[]{:S(2)}, u32[]{:S(2)}) async-start(f32[16,2,10,128]{3,1,2,0:T(2,128)} %copy.48), calls=%async_computation | async-start | bytes 327680 | tf_op jit(solution)/shard_map/all_to_all | solution.py:277
  61.2 0.1 copy.46
  61.3 0.2 pad_maximum_fusion.1
  61.4 5.5 copy.43.meta_ref
  67.1 0.1 copy.47
  67.2 0.1 stack_reshape.22
  67.2 0.1 copy.45
  67.3 0.1 stack_reshape.21
  67.5 0.6 pad_add_fusion.sc_ref
  68.0 3.5 all-to-all-done
  71.5 0.1 fusion.42
  71.7 0.2 pad_maximum_fusion.2
  71.8 5.5 copy.49.meta_ref
  77.4 58.9 %all-gather.6.cloned.1.call-done.w1_ref = bf16[64,512,256]{2,1,0:T(8,128)(2,1)} async-done(((bf16[4,512,256]{2,1,0:T(8,128)(2,1)}), bf16[64,512,256]{2,1,0:T(8,128)(2,1)}) %all-gather.6.cloned.1.call-update) | async-done | bytes 16777232 | tf_op jit(solution)/shard_map/all_gather | solution.py:253
  136.3 127.0 %all-gather.8.cloned.1.call-done.w2_ref = bf16[64,256,512]{2,1,0:T(8,128)(2,1)} async-done(((bf16[4,256,512]{2,1,0:T(8,128)(2,1)}), bf16[64,256,512]{2,1,0:T(8,128)(2,1)}) %all-gather.8.cloned.1.call-update) | async-done | bytes 16777232 | tf_op jit(solution)/shard_map/all_gather | solution.py:254
  263.2 104.6 %token_pass.1 = (bf16[1024,512]{1,0:T(8,128)(2,1)}, bf16[1024,512]{1,0:T(8,128)(2,1)}, f32[1024,128]{1,0:T(8,128)}) custom-call(s32[3,64]{1,0:T(4,128)} %pad_add_fusion.sc_ref, s32[8192]{0:T(1024)} %get-tuple-element.47.pos_ref, f32[20480,2]{1,0:T(8,128)} %copy.43.meta_ref, bf16[1024,512]{1,0:T(8,128)(2,1)} %x_ref.1, bf16[1024,512]{1,0:T(8,128)(2,1)} %dy_ref.1, ...), custom_call_target="tpu_custom_call" | custom-call | flops 60000002048 | bytes 40000000 | tf_op jit(solution)/shard_map/token_pass/pallas_call | solution.py:113
  367.8 1.8 copy.50
  369.6 20.2 %all-gather.10.cloned.1.call-done.x_ref = bf16[16384,512]{1,0:T(8,128)(2,1)} async-done(((bf16[1024,512]{1,0:T(8,128)(2,1)}), bf16[16384,512]{1,0:T(8,128)(2,1)}) %all-gather.10.cloned.1.call-update) | async-done | bytes 16777232 | tf_op jit(solution)/shard_map/all_gather | solution.py:278
  389.9 126.5 %all-gather.12.cloned.1.call-done.dy_ref = bf16[16384,512]{1,0:T(8,128)(2,1)} async-done(((bf16[1024,512]{1,0:T(8,128)(2,1)}), bf16[16384,512]{1,0:T(8,128)(2,1)}) %all-gather.12.cloned.1.call-update) | async-done | bytes 16777232 | tf_op jit(solution)/shard_map/all_gather | solution.py:279
  516.3 4.0 copy-done
  520.3 1.2 copy-done.2
  521.5 80.4 %owner_pass.1 = (bf16[4,512,256]{2,1,0:T(8,128)(2,1)}, bf16[4,256,512]{2,1,0:T(8,128)(2,1)}) custom-call(s32[2,64]{1,0:T(2,128)S(1)} %pad_add_fusion.1.sc_ref, f32[20480,2]{1,0:T(8,128)S(1)} %copy-done, bf16[16384,512]{1,0:T(8,128)(2,1)} %all-gather.10.cloned.1.call-done.x_ref, bf16[16384,512]{1,0:T(8,128)(2,1)} %all-gather.12.cloned.1.call-done.dy_ref, ...), custom_call_target="tpu_custom_call" | custom-call | flops 49999998976 | bytes 50000000 | tf_op jit(solution)/shard_map/owner_pass/pallas_call | solution.py:177
  (39 shorter events, 0.7 us)
Async XLA Ops:
  7.2 2.8 copy-start.3
  7.2 129.1 %all-gather.6.cloned.1.call-start = ((), (), s32[]{:S(2)}) async-start(), calls=%async_computation.1 | async-start | bytes 17825792 | tf_op jit(solution)/shard_map/all_gather | solution.py:253
  7.9 20.8 %copy-start.4 = (f32[1024,8]{0,1:T(8,128)S(1)}, f32[1024,8]{0,1:T(8,128)}, u32[]{:S(2)}) copy-start(f32[1024,8]{0,1:T(8,128)} %param.8) | copy-start | bytes 98308
  7.9 255.3 %all-gather.8.cloned.1.call-start = ((), (), s32[]{:S(2)}) async-start(), calls=%async_computation.2 | async-start | bytes 17825792 | tf_op jit(solution)/shard_map/all_gather | solution.py:254
  8.7 381.2 %all-gather.10.cloned.1.call-start = ((), (), s32[]{:S(2)}) async-start(), calls=%async_computation.3 | async-start | bytes 17825792 | tf_op jit(solution)/shard_map/all_gather | solution.py:278
  9.4 506.9 %all-gather.12.cloned.1.call-start = ((), (), s32[]{:S(2)}) async-start(), calls=%async_computation.4 | async-start | bytes 17825792 | tf_op jit(solution)/shard_map/all_gather | solution.py:279
  51.2 20.4 %all-to-all-start = ((f32[16,2,10,128]{3,1,2,0:T(2,128)}), f32[16,2,10,128]{3,1,2,0:T(2,128)S(1)}, u32[]{:S(2)}, u32[]{:S(2)}) async-start(f32[16,2,10,128]{3,1,2,0:T(2,128)} %copy.48), calls=%async_computation | async-start | bytes 327680 | tf_op jit(solution)/shard_map/all_to_all | solution.py:277
  263.2 253.1 %copy-start.1 = (bf16[4,512,256]{2,1,0:T(8,128)(2,1)S(1)}, bf16[4,512,256]{2,1,0:T(8,128)(2,1)}, u32[]{:S(2)}) copy-start(bf16[4,512,256]{2,1,0:T(8,128)(2,1)} %w1_ref.1) | copy-start | bytes 3145732
  516.3 4.0 copy-start
  520.3 1.2 copy-start.2
Sparse Core Ops, SparseCore 0:
  10.1 126.0 all-gather.5
  138.4 124.7 all-gather.7
  265.4 124.3 all-gather.9
  391.9 124.3 all-gather.11

commit v2 on v1

--- a/solution.py
+++ b/solution.py
@@ -7,12 +7,16 @@
 from jax.experimental.pallas import tpu as pltpu
 from jax.sharding import PartitionSpec as P
 
+
 CAP_NUM = 5
 CAP_DEN = 4
 PAIR_FACTOR = 2
 
 TILE = 128
-ALIGN = 8
+PICK_TILE = 256
+TOKEN_UNROLL = 2
+OWNER_UNROLL = 2
+ALIGN = 16
 LANES = 128
 TOKENS_PER_STEP = 16
 VMEM_BYTES = 62 * 1024 * 1024
@@ -50,39 +54,109 @@
     return jnp.where(tok == cols, 1.0, 0.0).astype(jnp.bfloat16)
 
 
-def token_kernel(zero_row, top_k, sc_ref, pos_ref, meta_ref, x_ref, dy_ref, w1_ref, w2_ref,
+def pick_kernel(n_ref, meta_ref, x_ref, dy_ref, rows_ref, drow_ref):
+    used = n_ref[pl.program_id(0)]
+
+    def tile(i, carry):
+        at = pl.ds(pl.multiple_of(i * PICK_TILE, PICK_TILE), PICK_TILE)
+        pick = pick_matrix(meta_ref[at, :], x_ref.shape[0])
+        rows_ref[at, :] = dot_nn(pick, x_ref[...]).astype(jnp.bfloat16)
+        drow_ref[at, :] = dot_nn(pick, dy_ref[...]).astype(jnp.bfloat16)
+        return carry
+
+    lax.fori_loop(0, (used + PICK_TILE - 1) // PICK_TILE, tile, 0)
+
+
+def pick_pass(used, meta, x, dy):
+    n_tokens, d = x.shape
+    dests = used.shape[0]
+    block_rows = meta.shape[0] // dests
+    whole = lambda e, *_: (0, 0)
+    row = lambda e, *_: (e, 0)
+    out = jax.ShapeDtypeStruct((meta.shape[0], d), jnp.bfloat16)
+    return pl.pallas_call(
+        pick_kernel,
+        out_shape=(out, out),
+        grid_spec=pltpu.PrefetchScalarGridSpec(
+            num_scalar_prefetch=1, grid=(dests,),
+            in_specs=[pl.BlockSpec((block_rows, 2), row),
+                      pl.BlockSpec((n_tokens, d), whole), pl.BlockSpec((n_tokens, d), whole)],
+            out_specs=[pl.BlockSpec((block_rows, d), row), pl.BlockSpec((block_rows, d), row)]),
+        compiler_params=pltpu.CompilerParams(dimension_semantics=("arbitrary",), vmem_limit_bytes=VMEM_BYTES // 2),
+        cost_estimate=pl.CostEstimate(flops=20_000_000_000, bytes_accessed=50_000_000, transcendentals=0),
+        name="pick_pass",
+    )(used, meta, x, dy)
+
+
+def out_product(act, w):
+    f = w.shape[1]
+    d = 2 * f
+    return jnp.concatenate([dot_nn(act, w[d:d + f, :]), dot_nn(act, w[d + f:d + 2 * f, :])], axis=1)
+
+
+def out_product_t(grad, w):
+    f = w.shape[1]
+    d = 2 * f
+    return dot_nt(grad[:, 0:f], w[d:d + f, :]) + dot_nt(grad[:, f:d], w[d + f:d + 2 * f, :])
+
+
+def tile_table(kept):
+    ends, total = [], 0
+    for k in kept:
+        total = total + (k + TILE - 1) // TILE
+        ends.append(total)
+
+    def find(i):
+        e, base, live_from = jnp.int32(0), jnp.int32(0), kept[0]
+        for n in range(1, len(kept)):
+            past = i >= ends[n - 1]
+            e = jnp.where(past, n, e)
+            base = jnp.where(past, ends[n - 1], base)
+            live_from = jnp.where(past, kept[n], live_from)
+        off = (i - base) * TILE
+        return e, off, live_from - off
+
+    return total, find
+
+
+def token_kernel(zero_row, top_k, sc_ref, src_ref, pos_ref, meta_ref, rows_ref, drow_ref, x_ref, dy_ref, w_ref,
                  y_ref, dx_ref, dg_ref, buf, dgb, tmp, tmpg):
-    e = pl.program_id(0)
+    g = pl.program_id(0)
     n_tokens, d = x_ref.shape
-
-    @pl.when(e == 0)
+    local_experts = w_ref.shape[0]
+    spare_row = zero_row + ALIGN
+
+    @pl.when(g == 0)
     def _():
         buf[pl.ds(zero_row, ALIGN), :] = jnp.zeros((ALIGN, 2 * d), jnp.float32)
         dgb[pl.ds(zero_row, ALIGN), :] = jnp.zeros((ALIGN, LANES), jnp.float32)
 
-    list_start, buf_start, kept = sc_ref[0, e], sc_ref[1, e], sc_ref[2, e]
-
-    def tile(i, carry):
-        meta = meta_ref[pl.ds(pl.multiple_of(list_start + i * TILE, ALIGN), TILE), :]
-        pick = pick_matrix(meta, n_tokens)
-        gate = meta[:, 1:2]
-        rows = dot_nn(pick, x_ref[...]).astype(jnp.bfloat16)
-        drow = dot_nn(pick, dy_ref[...])
-        act, slope = gelu_parts(dot_nn(rows, w1_ref[0]))
-        out = dot_nn(act.astype(jnp.bfloat16), w2_ref[0]).astype(jnp.bfloat16).astype(jnp.float32)
-        grad = (gate * drow).astype(jnp.bfloat16)
-        dact = dot_nt(grad, w2_ref[0]).astype(jnp.bfloat16).astype(jnp.float32)
-        dpre = (dact * slope).astype(jnp.bfloat16)
-        din = dot_nt(dpre, w1_ref[0]).astype(jnp.bfloat16).astype(jnp.float32)
-        at = pl.ds(pl.multiple_of(buf_start + i * TILE, ALIGN), TILE)
-        buf[at, 0:d] = gate * out
-        buf[at, d:2 * d] = din
-        dgb[at, :] = jnp.broadcast_to(jnp.sum(drow * out, axis=1, keepdims=True), (TILE, LANES))
+    first = g * local_experts
+    total, find = tile_table([sc_ref[2, first + n] for n in range(local_experts)])
+
+    def tiles(p, carry):
+        for u in range(TOKEN_UNROLL):
+            e, off, live = find(p * TOKEN_UNROLL + u)
+            real = live > 0
+            at = pl.ds(pl.multiple_of(jnp.where(real, sc_ref[0, first + e] + off, 0), ALIGN), TILE)
+            w = w_ref.at[e]
+            gate = meta_ref[at, 1:2]
+            drow = drow_ref[at, :].astype(jnp.float32)
+            act, slope = gelu_parts(dot_nn(rows_ref[at, :], w[0:d, :]))
+            out = out_product(act.astype(jnp.bfloat16), w).astype(jnp.bfloat16).astype(jnp.float32)
+            grad = (gate * drow).astype(jnp.bfloat16)
+            dact = out_product_t(grad, w).astype(jnp.bfloat16).astype(jnp.float32)
+            dpre = (dact * slope).astype(jnp.bfloat16)
+            din = dot_nt(dpre, w[0:d, :]).astype(jnp.bfloat16).astype(jnp.float32)
+            at = pl.ds(pl.multiple_of(jnp.where(real, sc_ref[1, first + e] + off, spare_row), ALIGN), TILE)
+            buf[at, 0:d] = gate * out
+            buf[at, d:2 * d] = din
+            dgb[at, :] = jnp.broadcast_to(jnp.sum(drow * out, axis=1, keepdims=True), (TILE, LANES))
         return carry
 
-    lax.fori_loop(0, (kept + TILE - 1) // TILE, tile, 0)
-
-    @pl.when(e == pl.num_programs(0) - 1)
+    lax.fori_loop(0, (total + TOKEN_UNROLL - 1) // TOKEN_UNROLL, tiles, 0)
+
+    @pl.when(g == pl.num_programs(0) - 1)
     def _():
         lane = lax.broadcasted_iota(jnp.int32, (1, LANES), 1)
 
@@ -105,23 +179,26 @@
         lax.fori_loop(0, n_tokens // TOKENS_PER_STEP, block, 0)
 
 
-def token_pass(scalars, pos, meta, block_rows, x, dy, w1, w2, buf_rows, zero_row, top_k):
+def token_pass(scalars, sources, pos, meta, rows, drow, x, dy, w_all, buf_rows, zero_row, top_k):
     n_tokens, d = x.shape
-    experts, _, f = w1.shape
-    per_dev = experts * block_rows // meta.shape[0]
+    experts = w_all.shape[0]
+    block_rows = meta.shape[0] // sources.shape[0]
+    per_dev = experts // sources.shape[0]
     whole = lambda e, *_: (0, 0)
+    dest = lambda g, sc, src, pos: (src[g], 0)
     return pl.pallas_call(
         functools.partial(token_kernel, zero_row, top_k),
         out_shape=(jax.ShapeDtypeStruct((n_tokens, d), jnp.bfloat16),
                    jax.ShapeDtypeStruct((n_tokens, d), jnp.bfloat16),
                    jax.ShapeDtypeStruct((n_tokens, LANES), jnp.float32)),
         grid_spec=pltpu.PrefetchScalarGridSpec(
-            num_scalar_prefetch=2, grid=(experts,),
-            in_specs=[pl.BlockSpec((block_rows, 2), lambda e, *_: (e // per_dev, 0)),
+            num_scalar_prefetch=3, grid=(experts // per_dev,),
+            in_specs=[pl.BlockSpec((block_rows, 2), dest),
+                      pl.BlockSpec((block_rows, d), dest),
+                      pl.BlockSpec((block_rows, d), dest),
                       pl.BlockSpec((n_tokens, d), whole, pipeline_mode=pl.Buffered(1)),
                       pl.BlockSpec((n_tokens, d), whole, pipeline_mode=pl.Buffered(1)),
-                      pl.BlockSpec((1, d, f), lambda e, *_: (e, 0, 0)),
-                      pl.BlockSpec((1, f, d), lambda e, *_: (e, 0, 0))],
+                      pl.BlockSpec((per_dev, *w_all.shape[1:]), lambda g, *_: (g, 0, 0))],
             out_specs=[pl.BlockSpec((n_tokens, d), whole, pipeline_mode=pl.Buffered(1)),
                        pl.BlockSpec((n_tokens, d), whole, pipeline_mode=pl.Buffered(1)),
                        pl.BlockSpec((n_tokens, LANES), whole, pipeline_mode=pl.Buffered(1))],
@@ -130,14 +207,14 @@
                             pltpu.VMEM((TOKENS_PER_STEP, 2 * d), jnp.float32),
                             pltpu.VMEM((TOKENS_PER_STEP, LANES), jnp.float32)]),
         compiler_params=pltpu.CompilerParams(dimension_semantics=("arbitrary",), vmem_limit_bytes=VMEM_BYTES),
-        cost_estimate=pl.CostEstimate(flops=60_000_000_000, bytes_accessed=40_000_000, transcendentals=4_000_000),
+        cost_estimate=pl.CostEstimate(flops=40_000_000_000, bytes_accessed=80_000_000, transcendentals=4_000_000),
         name="token_pass",
-    )(scalars, pos, meta, x, dy, w1, w2)
-
-
-def owner_kernel(sc_ref, meta_ref, x_ref, dy_ref, w1_ref, w2_ref, dw1_ref, dw2_ref, acc1, acc2):
+    )(scalars, sources, pos, meta, rows, drow, x, dy, w_all)
+
+
+def owner_kernel(sc_ref, meta_ref, xy_ref, w1_ref, w2_ref, dw1_ref, dw2_ref, acc1, acc2, rows_ref, grad_ref):
     s = pl.program_id(0)
-    n_tokens, d = x_ref.shape
+    n_tokens = xy_ref.shape[0] // 2
     local_experts = w1_ref.shape[0]
 
     @pl.when(s == 0)
@@ -145,24 +222,39 @@
         acc1[...] = jnp.zeros_like(acc1)
         acc2[...] = jnp.zeros_like(acc2)
 
-    for e in range(local_experts):
-        start, kept = sc_ref[0, s * local_experts + e], sc_ref[1, s * local_experts + e]
-
-        def tile(i, carry, e=e, start=start, kept=kept):
-            meta = meta_ref[pl.ds(pl.multiple_of(start + i * TILE, ALIGN), TILE), :]
-            pick = pick_matrix(meta, n_tokens)
-            live = lax.broadcasted_iota(jnp.int32, (TILE, 1), 0) + i * TILE < kept
-            gate = jnp.where(live, meta[:, 1:2], 0.0)
-            rows = dot_nn(pick, x_ref[...]).astype(jnp.bfloat16)
-            grad = (gate * dot_nn(pick, dy_ref[...])).astype(jnp.bfloat16)
+    last = s * local_experts + local_experts - 1
+    used = sc_ref[0, last] + sc_ref[1, last]
+
+    def pick_tile(i, carry):
+        at = pl.ds(pl.multiple_of(i * PICK_TILE, PICK_TILE), PICK_TILE)
+        meta = meta_ref[at, :]
+        pick = pick_matrix(meta, n_tokens)
+        rows_ref[at, :] = dot_nn(pick, xy_ref[0:n_tokens, :]).astype(jnp.bfloat16)
+        grad_ref[at, :] = (meta[:, 1:2] * dot_nn(pick, xy_ref[n_tokens:, :])).astype(jnp.bfloat16)
+        return carry
+
+    lax.fori_loop(0, (used + PICK_TILE - 1) // PICK_TILE, pick_tile, 0)
+
+    first = s * local_experts
+    total, find = tile_table([sc_ref[1, first + n] for n in range(local_experts)])
+
+    def tiles(p, carry):
+        for u in range(OWNER_UNROLL):
+            e, off, count = find(p * OWNER_UNROLL + u)
+            at = pl.ds(pl.multiple_of(jnp.where(count > 0, sc_ref[0, first + e] + off, 0), ALIGN), TILE)
+            live = lax.broadcasted_iota(jnp.int32, (TILE, 1), 0) < count
+            rows = rows_ref[at, :]
+            grad = jnp.where(live, grad_ref[at, :].astype(jnp.float32), 0.0).astype(jnp.bfloat16)
             act, slope = gelu_parts(dot_nn(rows, w1_ref[e]))
             dact = dot_nt(grad, w2_ref[e]).astype(jnp.bfloat16).astype(jnp.float32)
-            dpre = (dact * slope).astype(jnp.bfloat16)
-            acc2[e] += dot_tn(act.astype(jnp.bfloat16), grad)
+            dpre = jnp.where(live, dact * slope, 0.0).astype(jnp.bfloat16)
+            act = jnp.where(live, act, 0.0).astype(jnp.bfloat16)
+            rows = jnp.where(live, rows.astype(jnp.float32), 0.0).astype(jnp.bfloat16)
+            acc2[e] += dot_tn(act, grad)
             acc1[e] += dot_tn(rows, dpre)
-            return carry
-
-        lax.fori_loop(0, (kept + TILE - 1) // TILE, tile, 0)
+        return carry
+
+    lax.fori_loop(0, (total + OWNER_UNROLL - 1) // OWNER_UNROLL, tiles, 0)
 
     @pl.when(s == pl.num_programs(0) - 1)
     def _():
@@ -170,9 +262,8 @@
         dw2_ref[...] = acc2[...].astype(jnp.bfloat16)
 
 
-def owner_pass(scalars, meta, x_all, dy_all, w1, w2, sources):
-    local_experts, d, f = w1.shape
-    n_tokens = x_all.shape[0] // sources
+def owner_pass(scalars, meta, xy_all, w1, w2, sources):
+    _, d, _ = w1.shape
     block_rows = meta.shape[0] // sources
     return pl.pallas_call(
         owner_kernel,
@@ -180,17 +271,17 @@
         grid_spec=pltpu.PrefetchScalarGridSpec(
             num_scalar_prefetch=1, grid=(sources,),
             in_specs=[pl.BlockSpec((block_rows, 2), lambda s, *_: (s, 0)),
-                      pl.BlockSpec((n_tokens, d), lambda s, *_: (s, 0)),
-                      pl.BlockSpec((n_tokens, d), lambda s, *_: (s, 0)),
+                      pl.BlockSpec((xy_all.shape[0] // sources, d), lambda s, *_: (s, 0)),
                       pl.BlockSpec(w1.shape, lambda s, *_: (0, 0, 0)),
                       pl.BlockSpec(w2.shape, lambda s, *_: (0, 0, 0))],
             out_specs=[pl.BlockSpec(w1.shape, lambda s, *_: (0, 0, 0)),
                        pl.BlockSpec(w2.shape, lambda s, *_: (0, 0, 0))],
-            scratch_shapes=[pltpu.VMEM(w1.shape, jnp.float32), pltpu.VMEM(w2.shape, jnp.float32)]),
+            scratch_shapes=[pltpu.VMEM(w1.shape, jnp.float32), pltpu.VMEM(w2.shape, jnp.float32),
+                            pltpu.VMEM((block_rows, d), jnp.bfloat16), pltpu.VMEM((block_rows, d), jnp.bfloat16)]),
         compiler_params=pltpu.CompilerParams(dimension_semantics=("arbitrary",), vmem_limit_bytes=VMEM_BYTES // 2),
-        cost_estimate=pl.CostEstimate(flops=50_000_000_000, bytes_accessed=50_000_000, transcendentals=3_000_000),
+        cost_estimate=pl.CostEstimate(flops=60_000_000_000, bytes_accessed=50_000_000, transcendentals=3_000_000),
         name="owner_pass",
-    )(scalars, meta, x_all, dy_all, w1, w2)
+    )(scalars, meta, xy_all, w1, w2)
 
 
 def split3(v):
@@ -250,35 +341,44 @@
         list_rows = ceil_to(pair_cap + local_experts * (ALIGN - 1) + TILE, LANES)
         me = lax.axis_index('expert')
 
-        w1_all = lax.all_gather(w_in, 'expert', axis=0, tiled=True)
-        w2_all = lax.all_gather(w_out, 'expert', axis=0, tiled=True)
-
-        flat, hot, rank, counts, padded, local_start, tok_list, gate_list = route(
+        d_ff = w_in.shape[2]
+        xy = jnp.concatenate([x_in, grad_y], axis=0)
+        xy_all = lax.all_gather(xy, 'expert', axis=0, tiled=True)
+        w_all = jnp.concatenate([w_in, w_out[:, :, 0:d_ff], w_out[:, :, d_ff:]], axis=1)
+
+        _, hot, rank, counts, padded, local_start, tok_list, gate_list = route(
             expert_idx, gate_weight, num_experts, groups, list_rows)
-        counts_all = lax.all_gather(counts, 'expert')
+        count_plane = jnp.zeros((list_rows // LANES, LANES), jnp.float32).at[0, 0:num_experts].set(counts.astype(jnp.float32))
+        lists = jnp.stack([tok_list.reshape(groups, -1, LANES), gate_list.reshape(groups, -1, LANES),
+                           jnp.broadcast_to(count_plane, (groups, *count_plane.shape))], axis=1)
+        lists = lax.all_to_all(lists, 'expert', 0, 0, tiled=True)
+        counts_all = lists[:, 2, 0, 0:num_experts].astype(jnp.int32)
         before = jnp.cumsum(counts_all, axis=0) - counts_all
         kept_all = jnp.clip(capacity - before, 0, counts_all)
         kept_mine = lax.dynamic_index_in_dim(kept_all, me, 0, keepdims=False)
 
+        meta = columns(tok_list, gate_list)
+        used = jnp.sum(padded.reshape(groups, local_experts), axis=1)
+        rows, drow = pick_pass(used, meta, x_in, grad_y)
+
+        w_all = lax.all_gather(w_all, 'expert', axis=0, tiled=True)
         buf_start = jnp.cumsum(padded) - padded
         zero_row = n_pairs + num_experts * (ALIGN - 1) + TILE
-        buf_rows = zero_row + ALIGN
+        zero_row = ceil_to(zero_row, ALIGN)
+        buf_rows = zero_row + ALIGN + TILE
         pick = lambda v: jnp.sum(jnp.where(hot, v[None, :], 0), axis=1)
         pos = jnp.where(rank < pick(kept_mine), pick(buf_start) + rank, zero_row)
         token_scalars = jnp.stack([local_start, buf_start, kept_mine])
-        y_out, grad_x, grad_gate = token_pass(token_scalars, pos, columns(tok_list, gate_list), list_rows,
-                                              x_in, grad_y, w1_all, w2_all, buf_rows, zero_row, top_k)
 
         grid_all = ((counts_all + ALIGN - 1) // ALIGN * ALIGN).reshape(groups, groups, local_experts)
         start_all = jnp.cumsum(grid_all, axis=2) - grid_all
         start_own = lax.dynamic_index_in_dim(start_all, me, 1, keepdims=False).reshape(-1)
         kept_own = lax.dynamic_index_in_dim(kept_all.reshape(groups, groups, local_experts), me, 1, keepdims=False).reshape(-1)
-        lists = jnp.stack([tok_list.reshape(groups, -1, LANES), gate_list.reshape(groups, -1, LANES)], axis=1)
-        lists = lax.all_to_all(lists, 'expert', 0, 0, tiled=True)
-        x_all = lax.all_gather(x_in, 'expert', axis=0, tiled=True)
-        dy_all = lax.all_gather(grad_y, 'expert', axis=0, tiled=True)
         grad_w_in, grad_w_out = owner_pass(jnp.stack([start_own, kept_own]), columns(lists[:, 0], lists[:, 1]),
-                                           x_all, dy_all, w_in, w_out, groups)
+                                           xy_all, w_in, w_out, groups)
+        sources = jnp.arange(groups, dtype=jnp.int32)
+        y_out, grad_x, grad_gate = token_pass(token_scalars, sources, pos, meta, rows, drow,
+                                              x_in, grad_y, w_all, buf_rows, zero_row, top_k)
         return y_out, grad_x, grad_gate[:, :top_k], grad_w_in, grad_w_out
 
     return jax.shard_map(device_pass, mesh=mesh,

time: 612 us -> 463 us (0.76)
  the two profiles are of different devices: /device:TPU:15 before, /device:TPU:3 now
where the time goes in v2:
time: 463 us; the launch traced here: 462 us
  Pallas kernels  203 us (44%)
  waiting for transfers between devices  183 us (40%)
  local copies, waits for them, and re-layouts  26.8 us (6%)
  other arithmetic  25 us (5%)
  between operations  14.4 us (3%)
  starting transfers between devices  6.6 us (1%)
    all_gather x1, waiting for transfers between devices, device_pass(): xy_all = lax.all_gather(xy, 'expert', axis=0, tiled=True)  95.6 us
    pallas_call x1, Pallas kernels, owner_pass(): pl.pallas_call(owner_kernel, out_shape=(jax.ShapeDtypeStruct(w1.shape, jn...  93.2 us
    all_gather x1, waiting for transfers between devices, device_pass(): w_all = lax.all_gather(w_all, 'expert', axis=0, tiled=True)  87.4 us
    pallas_call x1, Pallas kernels, token_pass(): pl.pallas_call(functools.partial(token_kernel, zero_row, top_k), out_shap...  72.6 us
    pallas_call x1, Pallas kernels, pick_pass(): pl.pallas_call(pick_kernel, out_shape=(out, out), grid_spec=pltpu.Prefetc...  37.2 us
    unnamed x5, other arithmetic  13.3 us
    unnamed x20, local copies, waits for them, and re-layouts  11.4 us
    another operation x2, local copies, waits for them, and re-layouts, columns(): return jnp.stack([tokens.reshape(-1), gates.reshape(-1)], axis=1)  10.8 us
  transfers between devices with their start and end apart: 3, of which 2 were waited for; matrix products, arithmetic and copies ran while one was open for 9% of the time, Pallas kernels for 24%

profile of v2, /device:TPU:3, one launch (start us, length us, event | category | flops | bytes accessed | tf_op | source)
XLA Modules:
  0.0 462.2 jit_solution(14327332875219645498)
XLA Ops:
  7.2 1.4 fusion.49
  8.6 2.7 pad_maximum_fusion
  11.4 1.5 pad_maximum_fusion.1
  12.9 0.2 copy.60
  13.1 0.3 eq.55
  13.4 0.3 eq.59
  13.6 0.3 convert_reduce_fusion
  14.2 0.1 reshape.241
  14.3 0.1 sub.105
  14.4 0.1 fusion.46
  14.5 0.2 reduce_window_sum.56
  14.7 0.1 reduce_window_sum.57
  14.8 0.9 fusion.2
  15.7 0.2 copy.62
  15.9 0.3 reshape.242
  16.2 0.4 select_reduce_fusion.2
  16.7 2.7 fusion.3
  19.4 3.5 fusion.4
  23.0 3.5 fusion.5
  26.5 3.5 fusion.6
  30.0 3.8 fusion.7
  33.8 2.4 fusion
  36.4 0.9 copy.63
  37.3 6.5 %all-to-all-start = ((f32[16,3,10,128]{3,1,2,0:T(4,128)}), f32[16,3,10,128]{3,1,2,0:T(4,128)S(1)}, u32[]{:S(2)}, u32[]{:S(2)}) async-start(f32[16,3,10,128]{3,1,2,0:T(4,128)} %copy.63), calls=%async_computation | async-start | bytes 655360 | tf_op jit(solution)/shard_map/all_to_all | solution.py:354
  43.8 0.2 pad_maximum_fusion.3
  43.9 5.4 %copy.66.meta_ref = f32[20480,2]{1,0:T(8,128)} copy(f32[20480,2]{0,1:T(2,128)S(1)} %pad_maximum_fusion.3) | data formatting | bytes 327680 | tf_op jit(solution)/shard_map/stack | solution.py:325
  49.3 4.0 copy-done
  53.3 37.2 %pick_pass.1 = (bf16[20480,512]{1,0:T(8,128)(2,1)}, bf16[20480,512]{1,0:T(8,128)(2,1)}) custom-call(s32[16]{0:T(128)S(1)} %get-tuple-element.58.n_ref, f32[20480,2]{1,0:T(8,128)S(1)} %copy-done, bf16[1024,512]{1,0:T(8,128)(2,1)S(1)} %copy-done.3, bf16[1024,512]{1,0:T(8,128)(2,1)S(1)} %copy-done.4), custom_call_target="tpu_custom_call" | custom-call | flops 20000000000 | bytes 50000000 | tf_op jit(solution)/shard_map/pick_pass/pallas_call | solution.py:77
  90.5 0.2 reduce-window_clone.1
  90.8 0.1 copy.69
  91.0 0.1 copy.70
  91.1 0.1 stack_reshape.24
  91.3 0.1 copy.68
  91.4 0.1 stack_reshape.23
  91.5 0.1 fusion.50
  91.6 0.2 pad_maximum_fusion.4
  91.8 5.4 %copy.71.meta_ref = f32[20480,2]{1,0:T(8,128)} copy(f32[20480,2]{0,1:T(2,128)S(1)} %pad_maximum_fusion.4) | data formatting | bytes 327680 | tf_op jit(solution)/shard_map/stack | solution.py:325
  97.2 0.6 pad_add_fusion.sc_ref
  97.8 0.6 select_reduce_fusion.1
  98.4 0.6 add_select_fusion.6.pos_ref
  99.0 87.4 %all-gather.3.cloned.1.call-done.w_ref = bf16[64,1024,256]{2,1,0:T(8,128)(2,1)} async-done(((bf16[4,1024,256]{2,1,0:T(8,128)(2,1)}), bf16[64,1024,256]{2,1,0:T(8,128)(2,1)}) %all-gather.3.cloned.1.call-update) | async-done | bytes 33554448 | tf_op jit(solution)/shard_map/all_gather | solution.py:364
  186.4 0.5 iota.55.src_ref
  187.0 72.6 %token_pass.1 = (bf16[1024,512]{1,0:T(8,128)(2,1)}, bf16[1024,512]{1,0:T(8,128)(2,1)}, f32[1024,128]{1,0:T(8,128)}) custom-call(s32[3,64]{1,0:T(4,128)} %pad_add_fusion.sc_ref, s32[16]{0:T(128)} %iota.55.src_ref, s32[8192]{0:T(1024)} %add_select_fusion.6.pos_ref, f32[20480,2]{1,0:T(8,128)} %copy.66.meta_ref, bf16[20480,512]{1,0:T(8,128)(2,1)} %get-tuple-element.24.rows_ref, ...), custom_call_target="tpu_custom_call" | custom-call | flops 40000000000 | bytes 80000000 | tf_op jit(solution)/shard_map/token_pass/pallas_call | solution.py:189
  259.5 1.8 copy.72
  261.3 95.6 %all-gather.5.cloned.1.call-done.xy_ref = bf16[32768,512]{1,0:T(8,128)(2,1)} async-done(((bf16[2048,512]{1,0:T(8,128)(2,1)}), bf16[32768,512]{1,0:T(8,128)(2,1)}) %all-gather.5.cloned.1.call-update) | async-done | bytes 33554448 | tf_op jit(solution)/shard_map/all_gather | solution.py:346
  356.9 4.0 copy-done.1
  360.9 1.2 copy-done.5
  362.1 93.2 %owner_pass.1 = (bf16[4,512,256]{2,1,0:T(8,128)(2,1)}, bf16[4,256,512]{2,1,0:T(8,128)(2,1)}) custom-call(s32[2,64]{1,0:T(2,128)S(1)} %pad_add_fusion.1.sc_ref, f32[20480,2]{1,0:T(8,128)S(1)} %copy-done.1, bf16[32768,512]{1,0:T(8,128)(2,1)} %all-gather.5.cloned.1.call-done.xy_ref, bf16[4,512,256]{2,1,0:T(8,128)(2,1)S(1)} %copy-done.5, ...), custom_call_target="tpu_custom_call" | custom-call | flops 60000002048 | bytes 50000000 | tf_op jit(solution)/shard_map/owner_pass/pallas_call | solution.py:268
  (49 shorter events, 0.8 us)
Async XLA Ops:
  7.2 4.2 copy-start.3
  7.2 4.2 copy-start.4
  7.2 179.3 %all-gather.3.cloned.1.call-start = ((), (), s32[]{:S(2)}) async-start(), calls=%async_computation.1 | async-start | bytes 35651584 | tf_op jit(solution)/shard_map/all_gather | solution.py:364
  11.3 1.6 copy-start.6
  11.3 345.6 %all-gather.5.cloned.1.call-start = ((), (), s32[]{:S(2)}) async-start(), calls=%async_computation.2 | async-start | bytes 35651584 | tf_op jit(solution)/shard_map/all_gather | solution.py:346
  12.9 2.8 copy-start.7
  37.3 53.5 %all-to-all-start = ((f32[16,3,10,128]{3,1,2,0:T(4,128)}), f32[16,3,10,128]{3,1,2,0:T(4,128)S(1)}, u32[]{:S(2)}, u32[]{:S(2)}) async-start(f32[16,3,10,128]{3,1,2,0:T(4,128)} %copy.63), calls=%async_computation | async-start | bytes 655360 | tf_op jit(solution)/shard_map/all_to_all | solution.py:354
  49.3 4.0 copy-start
  187.0 170.0 %copy-start.2 = (bf16[4,256,512]{2,1,0:T(8,128)(2,1)S(1)}, bf16[4,256,512]{2,1,0:T(8,128)(2,1)}, u32[]{:S(2)}) copy-start(bf16[4,256,512]{2,1,0:T(8,128)(2,1)} %w2_ref.1) | copy-start | bytes 3145732
  356.9 4.0 copy-start.1
  360.9 1.2 copy-start.5
Sparse Core Ops, SparseCore 0:
  11.4 174.9 all-gather.2
  188.0 168.8 all-gather.4

commit v3 on v2

--- a/solution.py
+++ b/solution.py
@@ -15,7 +15,8 @@
 TILE = 128
 PICK_TILE = 256
 TOKEN_UNROLL = 2
-OWNER_UNROLL = 2
+OWNER_TILE = 256
+MOVE_ROWS = 64
 ALIGN = 16
 LANES = 128
 TOKENS_PER_STEP = 16
@@ -119,11 +120,31 @@
     return total, find
 
 
-def token_kernel(zero_row, top_k, sc_ref, src_ref, pos_ref, meta_ref, rows_ref, drow_ref, x_ref, dy_ref, w_ref,
-                 y_ref, dx_ref, dg_ref, buf, dgb, tmp, tmpg):
+def token_kernel(zero_row, top_k, slots, sc_ref, src_ref, pos_ref, meta_ref, rows_ref, drow_ref, x_ref, dy_ref, *refs):
+    w_refs, (y_ref, dx_ref, dg_ref, buf, dgb, tmp, tmpg, held, sems) = refs[:2 * slots], refs[2 * slots:]
     g = pl.program_id(0)
     n_tokens, d = x_ref.shape
-    local_experts = w_ref.shape[0]
+    half = held.shape[1] // 2
+    local_experts = 2 * half
+
+    def fetch(k, h):
+        return pltpu.make_async_copy(w_refs[2 * k + h], held.at[k % 2, pl.ds(h * half, half)], sems.at[k % 2, h])
+
+    @pl.when(g == 0)
+    def _():
+        for h in range(2):
+            fetch(0, h).start()
+
+    for k in range(slots):
+        @pl.when(g == k)
+        def _(k=k):
+            if k + 1 < slots:
+                for h in range(2):
+                    fetch(k + 1, h).start()
+            for h in range(2):
+                fetch(k, h).wait()
+
+    w_ref = held.at[g % 2]
     spare_row = zero_row + ALIGN
 
     @pl.when(g == 0)
@@ -179,48 +200,47 @@
         lax.fori_loop(0, n_tokens // TOKENS_PER_STEP, block, 0)
 
 
-def token_pass(scalars, sources, pos, meta, rows, drow, x, dy, w_all, buf_rows, zero_row, top_k):
+def token_pass(scalars, sources, pos, meta, rows, drow, x, dy, halves, buf_rows, zero_row, top_k):
     n_tokens, d = x.shape
-    experts = w_all.shape[0]
-    block_rows = meta.shape[0] // sources.shape[0]
-    per_dev = experts // sources.shape[0]
+    slots = len(halves)
+    half_shape = halves[0][0].shape
+    block_rows = meta.shape[0] // slots
     whole = lambda e, *_: (0, 0)
     dest = lambda g, sc, src, pos: (src[g], 0)
     return pl.pallas_call(
-        functools.partial(token_kernel, zero_row, top_k),
+        functools.partial(token_kernel, zero_row, top_k, slots),
         out_shape=(jax.ShapeDtypeStruct((n_tokens, d), jnp.bfloat16),
                    jax.ShapeDtypeStruct((n_tokens, d), jnp.bfloat16),
                    jax.ShapeDtypeStruct((n_tokens, LANES), jnp.float32)),
         grid_spec=pltpu.PrefetchScalarGridSpec(
-            num_scalar_prefetch=3, grid=(experts // per_dev,),
+            num_scalar_prefetch=3, grid=(slots,),
             in_specs=[pl.BlockSpec((block_rows, 2), dest),
                       pl.BlockSpec((block_rows, d), dest),
                       pl.BlockSpec((block_rows, d), dest),
                       pl.BlockSpec((n_tokens, d), whole, pipeline_mode=pl.Buffered(1)),
                       pl.BlockSpec((n_tokens, d), whole, pipeline_mode=pl.Buffered(1)),
-                      pl.BlockSpec((per_dev, *w_all.shape[1:]), lambda g, *_: (g, 0, 0))],
+                      *[pl.BlockSpec(memory_space=pl.ANY)] * (2 * slots)],
             out_specs=[pl.BlockSpec((n_tokens, d), whole, pipeline_mode=pl.Buffered(1)),
                        pl.BlockSpec((n_tokens, d), whole, pipeline_mode=pl.Buffered(1)),
                        pl.BlockSpec((n_tokens, LANES), whole, pipeline_mode=pl.Buffered(1))],
             scratch_shapes=[pltpu.VMEM((buf_rows, 2 * d), jnp.float32),
                             pltpu.VMEM((buf_rows, LANES), jnp.float32),
                             pltpu.VMEM((TOKENS_PER_STEP, 2 * d), jnp.float32),
-                            pltpu.VMEM((TOKENS_PER_STEP, LANES), jnp.float32)]),
+                            pltpu.VMEM((TOKENS_PER_STEP, LANES), jnp.float32),
+                            pltpu.VMEM((2, 2 * half_shape[0], *half_shape[1:]), jnp.bfloat16),
+                            pltpu.SemaphoreType.DMA((2, 2))]),
         compiler_params=pltpu.CompilerParams(dimension_semantics=("arbitrary",), vmem_limit_bytes=VMEM_BYTES),
         cost_estimate=pl.CostEstimate(flops=40_000_000_000, bytes_accessed=80_000_000, transcendentals=4_000_000),
         name="token_pass",
-    )(scalars, sources, pos, meta, rows, drow, x, dy, w_all)
-
-
-def owner_kernel(sc_ref, meta_ref, xy_ref, w1_ref, w2_ref, dw1_ref, dw2_ref, acc1, acc2, rows_ref, grad_ref):
+    )(scalars, sources, pos, meta, rows, drow, x, dy, *[h for pair in halves for h in pair])
+
+
+def owner_kernel(sc_ref, meta_ref, xy_ref, w1_ref, w2_ref, dw1_ref, dw2_ref, rows_ref, grad_ref, all_rows, all_grad,
+                 acc1, acc2):
     s = pl.program_id(0)
+    d = xy_ref.shape[1]
     n_tokens = xy_ref.shape[0] // 2
     local_experts = w1_ref.shape[0]
-
-    @pl.when(s == 0)
-    def _():
-        acc1[...] = jnp.zeros_like(acc1)
-        acc2[...] = jnp.zeros_like(acc2)
 
     last = s * local_experts + local_experts - 1
     used = sc_ref[0, last] + sc_ref[1, last]
@@ -235,36 +255,53 @@
 
     lax.fori_loop(0, (used + PICK_TILE - 1) // PICK_TILE, pick_tile, 0)
 
-    first = s * local_experts
-    total, find = tile_table([sc_ref[1, first + n] for n in range(local_experts)])
-
-    def tiles(p, carry):
-        for u in range(OWNER_UNROLL):
-            e, off, count = find(p * OWNER_UNROLL + u)
-            at = pl.ds(pl.multiple_of(jnp.where(count > 0, sc_ref[0, first + e] + off, 0), ALIGN), TILE)
-            live = lax.broadcasted_iota(jnp.int32, (TILE, 1), 0) < count
-            rows = rows_ref[at, :]
-            grad = jnp.where(live, grad_ref[at, :].astype(jnp.float32), 0.0).astype(jnp.bfloat16)
-            act, slope = gelu_parts(dot_nn(rows, w1_ref[e]))
-            dact = dot_nt(grad, w2_ref[e]).astype(jnp.bfloat16).astype(jnp.float32)
-            dpre = jnp.where(live, dact * slope, 0.0).astype(jnp.bfloat16)
-            act = jnp.where(live, act, 0.0).astype(jnp.bfloat16)
-            rows = jnp.where(live, rows.astype(jnp.float32), 0.0).astype(jnp.bfloat16)
-            acc2[e] += dot_tn(act, grad)
-            acc1[e] += dot_tn(rows, dpre)
-        return carry
-
-    lax.fori_loop(0, (total + OWNER_UNROLL - 1) // OWNER_UNROLL, tiles, 0)
+    for e in range(local_experts):
+        start, kept, base = (sc_ref[k, s * local_experts + e] for k in range(3))
+
+        def move(i, carry, e=e, start=start, kept=kept, base=base):
+            frm = pl.ds(pl.multiple_of(start + i * MOVE_ROWS, ALIGN), MOVE_ROWS)
+            to = pl.ds(pl.multiple_of(base + i * MOVE_ROWS, ALIGN), MOVE_ROWS)
+            live = lax.broadcasted_iota(jnp.int32, (MOVE_ROWS, 1), 0) + i * MOVE_ROWS < kept
+            all_rows[e, to, :] = jnp.where(live, rows_ref[frm, :], jnp.bfloat16(0))
+            all_grad[e, to, :] = jnp.where(live, grad_ref[frm, :], jnp.bfloat16(0))
+            return carry
+
+        lax.fori_loop(0, (kept + MOVE_ROWS - 1) // MOVE_ROWS, move, 0)
 
     @pl.when(s == pl.num_programs(0) - 1)
     def _():
-        dw1_ref[...] = acc1[...].astype(jnp.bfloat16)
-        dw2_ref[...] = acc2[...].astype(jnp.bfloat16)
-
-
-def owner_pass(scalars, meta, xy_all, w1, w2, sources):
-    _, d, _ = w1.shape
+        for e in range(local_experts):
+            count = (sc_ref[1, last - local_experts + 1 + e] + ALIGN - 1) // ALIGN * ALIGN
+            end = sc_ref[2, last - local_experts + 1 + e] + count
+
+            def clear(i, carry, e=e, end=end):
+                to = pl.ds(pl.multiple_of(end + i * MOVE_ROWS, ALIGN), MOVE_ROWS)
+                all_rows[e, to, :] = jnp.zeros((MOVE_ROWS, d), jnp.bfloat16)
+                all_grad[e, to, :] = jnp.zeros((MOVE_ROWS, d), jnp.bfloat16)
+                return carry
+
+            lax.fori_loop(0, OWNER_TILE // MOVE_ROWS, clear, 0)
+            acc1[...] = jnp.zeros_like(acc1)
+            acc2[...] = jnp.zeros_like(acc2)
+
+            def tile(i, carry, e=e):
+                at = pl.ds(pl.multiple_of(i * OWNER_TILE, OWNER_TILE), OWNER_TILE)
+                rows, grad = all_rows[e, at, :], all_grad[e, at, :]
+                act, slope = gelu_parts(dot_nn(rows, w1_ref[e]))
+                dact = dot_nt(grad, w2_ref[e]).astype(jnp.bfloat16).astype(jnp.float32)
+                acc2[...] += dot_tn(act.astype(jnp.bfloat16), grad)
+                acc1[...] += dot_tn(rows, (dact * slope).astype(jnp.bfloat16))
+                return carry
+
+            lax.fori_loop(0, (end + OWNER_TILE - 1) // OWNER_TILE, tile, 0)
+            dw1_ref[e] = acc1[...].astype(jnp.bfloat16)
+            dw2_ref[e] = acc2[...].astype(jnp.bfloat16)
+
+
+def owner_pass(scalars, meta, xy_all, w1, w2, sources, capacity):
+    local_experts, d, _ = w1.shape
     block_rows = meta.shape[0] // sources
+    all_rows = ceil_to(capacity + sources * ALIGN + OWNER_TILE, OWNER_TILE)
     return pl.pallas_call(
         owner_kernel,
         out_shape=(jax.ShapeDtypeStruct(w1.shape, jnp.bfloat16), jax.ShapeDtypeStruct(w2.shape, jnp.bfloat16)),
@@ -276,9 +313,11 @@
                       pl.BlockSpec(w2.shape, lambda s, *_: (0, 0, 0))],
             out_specs=[pl.BlockSpec(w1.shape, lambda s, *_: (0, 0, 0)),
                        pl.BlockSpec(w2.shape, lambda s, *_: (0, 0, 0))],
-            scratch_shapes=[pltpu.VMEM(w1.shape, jnp.float32), pltpu.VMEM(w2.shape, jnp.float32),
-                            pltpu.VMEM((block_rows, d), jnp.bfloat16), pltpu.VMEM((block_rows, d), jnp.bfloat16)]),
-        compiler_params=pltpu.CompilerParams(dimension_semantics=("arbitrary",), vmem_limit_bytes=VMEM_BYTES // 2),
+            scratch_shapes=[pltpu.VMEM((block_rows, d), jnp.bfloat16), pltpu.VMEM((block_rows, d), jnp.bfloat16),
+                            pltpu.VMEM((local_experts, all_rows, d), jnp.bfloat16),
+                            pltpu.VMEM((local_experts, all_rows, d), jnp.bfloat16),
+                            pltpu.VMEM(w1.shape[1:], jnp.float32), pltpu.VMEM(w2.shape[1:], jnp.float32)]),
+        compiler_params=pltpu.CompilerParams(dimension_semantics=("arbitrary",), vmem_limit_bytes=VMEM_BYTES),
         cost_estimate=pl.CostEstimate(flops=60_000_000_000, bytes_accessed=50_000_000, transcendentals=3_000_000),
         name="owner_pass",
     )(scalars, meta, xy_all, w1, w2)
@@ -325,6 +364,23 @@
     return jnp.stack([tokens.reshape(-1), gates.reshape(-1)], axis=1)
 
 
+def mesh_moves(z_size, y_size):
+    cores = 2
+    size = z_size * y_size * cores
+
+    def along(move):
+        pairs = []
+        for i in range(size):
+            z, y, c = move(i // (y_size * cores), (i // cores) % y_size, i % cores)
+            pairs.append((i, (z * y_size + y) * cores + c))
+        return lambda v: lax.ppermute(v, 'expert', pairs)
+
+    z_by = {k: along(lambda z, y, c, k=k: ((z + k) % z_size, y, c)) for k in range(1, z_size)}
+    y_swap = along(lambda z, y, c: (z, 1 - y, c))
+    c_swap = along(lambda z, y, c: (z, y, 1 - c))
+    return z_by, y_swap, c_swap, lambda v: lax.ppermute(v, 'data', [(0, 1), (1, 0)])
+
+
 def solution(mesh):
     groups = mesh.shape['expert']
     tok_spec = P(('data', 'expert'), None)
@@ -342,12 +398,23 @@
         me = lax.axis_index('expert')
 
         d_ff = w_in.shape[2]
-        xy = jnp.concatenate([x_in, grad_y], axis=0)
-        xy_all = lax.all_gather(xy, 'expert', axis=0, tiled=True)
-        w_all = jnp.concatenate([w_in, w_out[:, :, 0:d_ff], w_out[:, :, d_ff:]], axis=1)
-
+        half = local_experts // 2
+        my_data = lax.axis_index('data')
+        w_own = jnp.concatenate([w_in, w_out[:, :, 0:d_ff], w_out[:, :, d_ff:]], axis=1)
+        ring = lax.dynamic_slice_in_dim(w_own, my_data * half, half, axis=0)
+        other = lax.dynamic_slice_in_dim(w_own, (1 - my_data) * half, half, axis=0)
+        z_by, y_swap, c_swap, x_swap = mesh_moves(groups // 4, 2)
+        near, z1, z3 = y_swap(ring), z_by[1](ring), z_by[3](ring)
         _, hot, rank, counts, padded, local_start, tok_list, gate_list = route(
             expert_idx, gate_weight, num_experts, groups, list_rows)
+        near, z1, z3, ring_late, tok_list, gate_list = lax.optimization_barrier((near, z1, z3, ring, tok_list, gate_list))
+        z2 = z_by[2](ring_late)
+        near_x = x_swap(near)
+        z1_x = x_swap(z1)
+        z3_x = x_swap(z3)
+        z1_y, z3_y = y_swap(z1), y_swap(z3)
+        xy = jnp.concatenate([x_in, grad_y], axis=0)
+
         count_plane = jnp.zeros((list_rows // LANES, LANES), jnp.float32).at[0, 0:num_experts].set(counts.astype(jnp.float32))
         lists = jnp.stack([tok_list.reshape(groups, -1, LANES), gate_list.reshape(groups, -1, LANES),
                            jnp.broadcast_to(count_plane, (groups, *count_plane.shape))], axis=1)
@@ -360,25 +427,43 @@
         meta = columns(tok_list, gate_list)
         used = jnp.sum(padded.reshape(groups, local_experts), axis=1)
         rows, drow = pick_pass(used, meta, x_in, grad_y)
-
-        w_all = lax.all_gather(w_all, 'expert', axis=0, tiled=True)
-        buf_start = jnp.cumsum(padded) - padded
+        z1_y, z3_y, z2, rows, drow = lax.optimization_barrier((z1_y, z3_y, z2, rows, drow))
+        z2_y = y_swap(z2)
+        xy, _ = lax.optimization_barrier((xy, rows))
+        xy_all = lax.all_gather(xy, 'expert', axis=0, tiled=True)
+        halves, where = [], []
+        for at, v, u in [((0, 0), ring, other), ((0, 1), near, near_x), ((1, 0), z1, z1_x), ((3, 0), z3, z3_x),
+                         ((1, 1), z1_y, x_swap(z1_y)), ((3, 1), z3_y, x_swap(z3_y)),
+                         ((2, 0), z2, x_swap(z2)), ((2, 1), z2_y, x_swap(z2_y))]:
+            halves += [(v, u), (c_swap(v), c_swap(u))]
+            where += [(*at, 0), (*at, 1)]
+
+        z, y, c = me // 4, (me // 2) % 2, me % 2
+        sources = jnp.stack([((z - dz) % 4) * 4 + (y ^ dy) * 2 + (c ^ dc) for dz, dy, dc in where]).astype(jnp.int32)
+        order = (sources[:, None] * local_experts
+                 + (jnp.arange(local_experts, dtype=jnp.int32) + half * my_data) % local_experts).reshape(num_experts)
+        slot_hot = order[:, None] == jnp.arange(num_experts, dtype=jnp.int32)[None, :]
+        by_slot = lambda v: jnp.sum(jnp.where(slot_hot, v[None, :], 0), axis=1)
+        padded_slot = by_slot(padded)
+        slot_start = jnp.cumsum(padded_slot) - padded_slot
+        buf_start = jnp.sum(jnp.where(slot_hot, slot_start[:, None], 0), axis=0)
         zero_row = n_pairs + num_experts * (ALIGN - 1) + TILE
         zero_row = ceil_to(zero_row, ALIGN)
         buf_rows = zero_row + ALIGN + TILE
         pick = lambda v: jnp.sum(jnp.where(hot, v[None, :], 0), axis=1)
         pos = jnp.where(rank < pick(kept_mine), pick(buf_start) + rank, zero_row)
-        token_scalars = jnp.stack([local_start, buf_start, kept_mine])
+        token_scalars = jnp.stack([by_slot(local_start), slot_start, by_slot(kept_mine)])
 
         grid_all = ((counts_all + ALIGN - 1) // ALIGN * ALIGN).reshape(groups, groups, local_experts)
         start_all = jnp.cumsum(grid_all, axis=2) - grid_all
         start_own = lax.dynamic_index_in_dim(start_all, me, 1, keepdims=False).reshape(-1)
         kept_own = lax.dynamic_index_in_dim(kept_all.reshape(groups, groups, local_experts), me, 1, keepdims=False).reshape(-1)
-        grad_w_in, grad_w_out = owner_pass(jnp.stack([start_own, kept_own]), columns(lists[:, 0], lists[:, 1]),
-                                           xy_all, w_in, w_out, groups)
-        sources = jnp.arange(groups, dtype=jnp.int32)
+        kept_rows = (kept_own.reshape(groups, local_experts) + ALIGN - 1) // ALIGN * ALIGN
+        base_own = (jnp.cumsum(kept_rows, axis=0) - kept_rows).reshape(-1)
+        grad_w_in, grad_w_out = owner_pass(jnp.stack([start_own, kept_own, base_own]), columns(lists[:, 0], lists[:, 1]),
+                                           xy_all, w_in, w_out, groups, capacity)
         y_out, grad_x, grad_gate = token_pass(token_scalars, sources, pos, meta, rows, drow,
-                                              x_in, grad_y, w_all, buf_rows, zero_row, top_k)
+                                              x_in, grad_y, halves, buf_rows, zero_row, top_k)
         return y_out, grad_x, grad_gate[:, :top_k], grad_w_in, grad_w_out
 
     return jax.shard_map(device_pass, mesh=mesh,

time: 463 us -> 474 us (1.024)
  Pallas kernels: 203 us -> 181 us
  starting transfers between devices: 6.6 us -> 27 us
  waiting for transfers between devices: 183 us -> 198 us
    ppermute x0 -> x30, waiting for transfers between devices: none -> 153 us  [the longest x7 125 us: mesh_moves(): lax.ppermute(v, 'data', [(0, 1), (1, 0)])]
    all_gather x1, waiting for transfers between devices: 95.6 us -> 0.01 us  [device_pass(): xy_all = lax.all_gather(xy, 'expert', axis=0, tiled=True)]
    all_gather x1 -> x0, waiting for transfers between devices: 87.4 us -> none  [device_pass(): w_all = lax.all_gather(w_all, 'expert', axis=0, tiled=True)]
    all_to_all x1, waiting for transfers between devices: 0.01 us -> 45.6 us  [device_pass(): lists = lax.all_to_all(lists, 'expert', 0, 0, tiled=True)]
    pallas_call x1, Pallas kernels: 93.2 us -> 69 us  [owner_pass(): pl.pallas_call(owner_kernel, out_shape=(jax.ShapeDtypeStruct(w1.shape, jn...]
    ppermute x0 -> x30, starting transfers between devices: none -> 22.8 us  [the longest x23 19 us: along(): return lambda v: lax.ppermute(v, 'expert', pairs)]
    unnamed x20 -> x30, local copies, waits for them, and re-layouts: 11.4 us -> 7.04 us
  transfers between devices with their start and end apart: 3 -> 32, of which waited for: 2 -> 12; matrix products, arithmetic and copies ran while one was open for 9% -> 8% of each run, Pallas kernels for 24% -> 24%
where the time goes in v3:
time: 474 us; the launch traced here: 473 us
  waiting for transfers between devices  198 us (42%)
  Pallas kernels  181 us (38%)
  starting transfers between devices  27 us (6%)
  other arithmetic  25.6 us (5%)
  local copies, waits for them, and re-layouts  23.6 us (5%)
  between operations  14.6 us (3%)
    ppermute x7, waiting for transfers between devices, mesh_moves(): lax.ppermute(v, 'data', [(0, 1), (1, 0)])  125 us
    pallas_call x1, Pallas kernels, token_pass(): pl.pallas_call(functools.partial(token_kernel, zero_row, top_k, slots), o...  74.6 us
    pallas_call x1, Pallas kernels, owner_pass(): pl.pallas_call(owner_kernel, out_shape=(jax.ShapeDtypeStruct(w1.shape, jn...  69 us
    all_to_all x1, waiting for transfers between devices, device_pass(): lists = lax.all_to_all(lists, 'expert', 0, 0, tiled=True)  45.6 us
    pallas_call x1, Pallas kernels, pick_pass(): pl.pallas_call(pick_kernel, out_shape=(out, out), grid_spec=pltpu.Prefetc...  37.2 us
    ppermute x23, waiting for transfers between devices, along(): return lambda v: lax.ppermute(v, 'expert', pairs)  27.7 us
    ppermute x23, starting transfers between devices, along(): return lambda v: lax.ppermute(v, 'expert', pairs)  19 us
    unnamed x5, other arithmetic  13.3 us
  transfers between devices with their start and end apart: 32, of which 12 were waited for; matrix products, arithmetic and copies ran while one was open for 8% of the time, Pallas kernels for 24%

profile of v3, /device:TPU:3, one launch (start us, length us, event | category | flops | bytes accessed | tf_op | source)
XLA Modules:
  0.0 472.9 jit_solution(11595712886765906983)
XLA Ops:
  7.2 1.3 fusion.54
  8.5 1.4 pad_maximum_fusion
  9.9 1.1 constant_dynamic-slice_fusion.2
  11.0 1.2 collective-permute-start
  12.2 1.3 collective-permute-start.1
  13.5 2.0 collective-permute-start.2
  17.4 0.9 fusion.2
  19.3 2.7 fusion.3
  22.1 3.5 fusion.4
  25.6 3.5 fusion.5
  29.2 3.5 fusion.6
  32.7 3.8 fusion.7
  36.5 2.4 fusion
  39.0 1.5 pad_maximum_fusion.1
  40.5 20.3 %collective-permute-done.2.refs_12_ = bf16[2,1024,256]{2,1,0:T(8,128)(2,1)} collective-permute-done((bf16[2,1024,256]{2,1,0:T(8,128)(2,1)}, bf16[2,1024,256]{2,1,0:T(8,128)(2,1)}, u32[]{:S(2)}, u32[]{:S(2)}) %collective-permute-start.2) | collective-permute-done | bytes 1048608 | tf_op jit(solution)/shard_map/ppermute | solution.py:376
  61.0 5.5 %copy.91.meta_ref = f32[20480,2]{1,0:T(8,128)} copy(f32[20480,2]{0,1:T(2,128)S(1)} %pad_maximum_fusion.3) | data formatting | bytes 327680 | tf_op jit(solution)/shard_map/stack | solution.py:364
  66.7 1.2 collective-permute-start.4
  68.4 4.0 copy-done
  72.4 37.2 %pick_pass.1 = (bf16[20480,512]{1,0:T(8,128)(2,1)}, bf16[20480,512]{1,0:T(8,128)(2,1)}) custom-call(s32[16]{0:T(128)S(1)} %get-tuple-element.87.n_ref, f32[20480,2]{1,0:T(8,128)S(1)} %copy-done, bf16[1024,512]{1,0:T(8,128)(2,1)S(1)} %copy-done.1, bf16[1024,512]{1,0:T(8,128)(2,1)S(1)} %copy-done.2), custom_call_target="tpu_custom_call" | custom-call | flops 20000000000 | bytes 50000000 | tf_op jit(solution)/shard_map/pick_pass/pallas_call | solution.py:78
  109.6 3.3 collective-permute-done.4.refs_20_
  112.9 2.6 collective-permute-done.5.refs_24_
  115.6 1.8 collective-permute-start.6
  117.7 0.7 collective-permute-start.9
  118.4 1.2 collective-permute-start.11
  120.2 1.1 collective-permute-done.7.refs_3_
  121.6 0.8 copy-done.9
  122.4 19.7 %collective-permute-done.8.refs_5_ = bf16[2,1024,256]{2,1,0:T(8,128)(2,1)S(1)} collective-permute-done((bf16[2,1024,256]{2,1,0:T(8,128)(2,1)}, bf16[2,1024,256]{2,1,0:T(8,128)(2,1)S(1)}, u32[]{:S(2)}, u32[]{:S(2)}) %collective-permute-start.8) | collective-permute-done | bytes 1048608 | tf_op jit(solution)/shard_map/ppermute | solution.py:381
  142.0 2.1 collective-permute-start.15
  144.3 0.7 fusion.45
  145.1 19.4 %collective-permute-done.11.refs_9_ = bf16[2,1024,256]{2,1,0:T(8,128)(2,1)} collective-permute-done((bf16[2,1024,256]{2,1,0:T(8,128)(2,1)}, bf16[2,1024,256]{2,1,0:T(8,128)(2,1)}, u32[]{:S(2)}, u32[]{:S(2)}) %collective-permute-start.11) | collective-permute-done | bytes 1048608 | tf_op jit(solution)/shard_map/ppermute | solution.py:381
  164.7 2.4 collective-permute-start.18
  167.2 19.8 %collective-permute-done.14.refs_13_ = bf16[2,1024,256]{2,1,0:T(8,128)(2,1)S(1)} collective-permute-done((bf16[2,1024,256]{2,1,0:T(8,128)(2,1)}, bf16[2,1024,256]{2,1,0:T(8,128)(2,1)S(1)}, u32[]{:S(2)}, u32[]{:S(2)}) %collective-permute-start.14) | collective-permute-done | bytes 1048608 | tf_op jit(solution)/shard_map/ppermute | solution.py:381
  187.2 2.3 collective-permute-start.13
  189.7 0.9 copy.88
  190.6 4.2 all-to-all-start
  195.5 45.6 %all-to-all-done = f32[16,3,10,128]{3,1,2,0:T(4,128)S(1)} async-done(((f32[16,3,10,128]{3,1,2,0:T(4,128)}), f32[16,3,10,128]{3,1,2,0:T(4,128)S(1)}, u32[]{:S(2)}, u32[]{:S(2)}) %all-to-all-start) | async-done | bytes 245792 | tf_op jit(solution)/shard_map/all_to_all | solution.py:421
  241.5 1.3 collective-permute-start.23
  242.8 0.7 collective-permute-start.24
  244.4 22.2 %collective-permute-done.20.refs_21_ = bf16[2,1024,256]{2,1,0:T(8,128)(2,1)} collective-permute-done((bf16[2,1024,256]{2,1,0:T(8,128)(2,1)}, bf16[2,1024,256]{2,1,0:T(8,128)(2,1)}, u32[]{:S(2)}, u32[]{:S(2)}) %collective-permute-start.20) | collective-permute-done | bytes 1048608 | tf_op jit(solution)/shard_map/ppermute | solution.py:381
  267.2 21.9 %collective-permute-done.23.refs_25_ = bf16[2,1024,256]{2,1,0:T(8,128)(2,1)} collective-permute-done((bf16[2,1024,256]{2,1,0:T(8,128)(2,1)}, bf16[2,1024,256]{2,1,0:T(8,128)(2,1)}, u32[]{:S(2)}, u32[]{:S(2)}) %collective-permute-start.23) | collective-permute-done | bytes 1048608 | tf_op jit(solution)/shard_map/ppermute | solution.py:381
  289.7 21.9 %collective-permute-done.27.refs_29_ = bf16[2,1024,256]{2,1,0:T(8,128)(2,1)} collective-permute-done((bf16[2,1024,256]{2,1,0:T(8,128)(2,1)}, bf16[2,1024,256]{2,1,0:T(8,128)(2,1)}, u32[]{:S(2)}, u32[]{:S(2)}) %collective-permute-start.27) | collective-permute-done | bytes 1048608 | tf_op jit(solution)/shard_map/ppermute | solution.py:381
  312.6 5.4 %copy.100.meta_ref = f32[20480,2]{1,0:T(8,128)} copy(f32[20480,2]{0,1:T(2,128)S(1)} %pad_maximum_fusion.4) | data formatting | bytes 327680 | tf_op jit(solution)/shard_map/stack | solution.py:364
  318.0 0.6 pad_add_fusion.1.sc_ref
  318.8 0.6 pad_add_fusion.sc_ref
  320.0 0.6 add_select_fusion.6.pos_ref
  320.7 74.6 %token_pass.1 = (bf16[1024,512]{1,0:T(8,128)(2,1)}, bf16[1024,512]{1,0:T(8,128)(2,1)}, f32[1024,128]{1,0:T(8,128)}) custom-call(s32[3,64]{1,0:T(4,128)} %pad_add_fusion.sc_ref, s32[16]{0:T(128)} %copy-done.7, s32[8192]{0:T(1024)} %add_select_fusion.6.pos_ref, f32[20480,2]{1,0:T(8,128)} %copy.91.meta_ref, bf16[20480,512]{1,0:T(8,128)(2,1)} %get-tuple-element.43.rows_ref, ...), custom_call_target="tpu_custom_call" | custom-call | flops 40000000000 | bytes 80000000 | tf_op jit(solution)/shard_map/token_pass/pallas_call | solution.py:210
  395.3 1.8 copy.101
  397.1 69.0 %owner_pass.1 = (bf16[4,512,256]{2,1,0:T(8,128)(2,1)}, bf16[4,256,512]{2,1,0:T(8,128)(2,1)}) custom-call(s32[3,64]{1,0:T(4,128)} %pad_add_fusion.1.sc_ref, f32[20480,2]{1,0:T(8,128)} %copy.100.meta_ref, bf16[32768,512]{1,0:T(8,128)(2,1)} %all-gather.2.cloned.1.call-done.xy_ref, bf16[4,512,256]{2,1,0:T(8,128)(2,1)} %w1_ref.1, bf16[4,256,512]{2,1,0:T(8,128)(2,1)} %w2_ref.1), custom_call_target="tpu_custom_call" | custom-call | flops 60000002048 | bytes 50000000 | tf_op jit(solution)/shard_map/owner_pass/pallas_call | solution.py:305
  (132 shorter events, 10.6 us)
Async XLA Ops:
  7.2 390.0 %all-gather.2.cloned.1.call-start = ((), (), s32[]{:S(2)}) async-start(), calls=%async_computation.1 | async-start | bytes 35651584 | tf_op jit(solution)/shard_map/all_gather | solution.py:433
  8.5 7.1 %copy-start.5 = (s32[1024,8]{0,1:T(8,128)S(1)}, s32[1024,8]{0,1:T(8,128)}, u32[]{:S(2)}) copy-start(s32[1024,8]{0,1:T(8,128)} %param.9) | copy-start | bytes 98308
  9.9 8.5 %copy-start.6 = (f32[1024,8]{0,1:T(8,128)S(1)}, f32[1024,8]{0,1:T(8,128)}, u32[]{:S(2)}) copy-start(f32[1024,8]{0,1:T(8,128)} %param.10) | copy-start | bytes 98308
  11.0 106.3 %copy-start.3 = (bf16[2,1024,256]{2,1,0:T(8,128)(2,1)}, bf16[2,1024,256]{2,1,0:T(8,128)(2,1)S(1)}, u32[]{:S(2)}) copy-start(bf16[2,1024,256]{2,1,0:T(8,128)(2,1)S(1)} %get-tuple-element.91.refs_1_) | copy-start | bytes 3145732
  11.0 29.5 %collective-permute-start = (bf16[2,1024,256]{2,1,0:T(8,128)(2,1)}, bf16[2,1024,256]{2,1,0:T(8,128)(2,1)}, u32[]{:S(2)}, u32[]{:S(2)}) collective-permute-start(bf16[2,1024,256]{2,1,0:T(8,128)(2,1)} %get-tuple-element.40.refs_0_), channel_id=1, source_target_pairs={{0,2},{1,3},{2,0},{3,1},{4,6},{5,7},{6,4},{7,5},{8,10},{9,11},{10,... | collective-permute-start | bytes 3145736 | tf_op jit(solution)/shard_map/ppermute | solution.py:376
  12.2 28.2 %collective-permute-start.1 = (bf16[2,1024,256]{2,1,0:T(8,128)(2,1)}, bf16[2,1024,256]{2,1,0:T(8,128)(2,1)}, u32[]{:S(2)}, u32[]{:S(2)}) collective-permute-start(bf16[2,1024,256]{2,1,0:T(8,128)(2,1)} %get-tuple-element.40.refs_0_), channel_id=1, source_target_pairs={{0,4},{1,5},{2,6},{3,7},{4,8},{5,9},{6,10},{7,11},{8,12},{9,13},{1... | collective-permute-start | bytes 3145736 | tf_op jit(solution)/shard_map/ppermute | solution.py:376
  13.5 47.3 %collective-permute-start.2 = (bf16[2,1024,256]{2,1,0:T(8,128)(2,1)}, bf16[2,1024,256]{2,1,0:T(8,128)(2,1)}, u32[]{:S(2)}, u32[]{:S(2)}) collective-permute-start(bf16[2,1024,256]{2,1,0:T(8,128)(2,1)} %get-tuple-element.40.refs_0_), channel_id=1, source_target_pairs={{0,12},{1,13},{2,14},{3,15},{4,0},{5,1},{6,2},{7,3},{8,4},{9,5},{1... | collective-permute-start | bytes 3145736 | tf_op jit(solution)/shard_map/ppermute | solution.py:376
  16.7 8.9 %copy-start.4 = (f32[32,64]{1,0:T(8,128)}, f32[32,64]{1,0:T(8,128)S(1)}, u32[]{:S(2)}) copy-start(f32[32,64]{1,0:T(8,128)S(1)} %reduce_window_sum.68) | copy-start | bytes 24580
  36.4 2.5 copy-start.1
  36.5 2.5 copy-start.2
  66.5 43.1 %collective-permute-start.3 = (bf16[2,1024,256]{2,1,0:T(8,128)(2,1)}, bf16[2,1024,256]{2,1,0:T(8,128)(2,1)}, u32[]{:S(2)}, u32[]{:S(2)}) collective-permute-start(bf16[2,1024,256]{2,1,0:T(8,128)(2,1)} %collective-permute-done.1.refs_8_), channel_id=1, source_target_pairs={{0,2},{1,3},{2,0},{3,1},{4,6},{5,7},{6,4},{7,5},{8,10},{9,11},{10,... | collective-permute-start | bytes 3145736 | tf_op jit(solution)/shard_map/ppermute | solution.py:376
  66.7 46.2 %collective-permute-start.4 = (bf16[2,1024,256]{2,1,0:T(8,128)(2,1)}, bf16[2,1024,256]{2,1,0:T(8,128)(2,1)}, u32[]{:S(2)}, u32[]{:S(2)}) collective-permute-start(bf16[2,1024,256]{2,1,0:T(8,128)(2,1)} %collective-permute-done.2.refs_12_), channel_id=1, source_target_pairs={{0,2},{1,3},{2,0},{3,1},{4,6},{5,7},{6,4},{7,5},{8,10},{9,11},{10,... | collective-permute-start | bytes 3145736 | tf_op jit(solution)/shard_map/ppermute | solution.py:376
  68.0 47.6 %collective-permute-start.5 = (bf16[2,1024,256]{2,1,0:T(8,128)(2,1)}, bf16[2,1024,256]{2,1,0:T(8,128)(2,1)}, u32[]{:S(2)}, u32[]{:S(2)}) collective-permute-start(bf16[2,1024,256]{2,1,0:T(8,128)(2,1)} %get-tuple-element.40.refs_0_), channel_id=1, source_target_pairs={{0,8},{1,9},{2,10},{3,11},{4,12},{5,13},{6,14},{7,15},{8,0},{9,1},... | collective-permute-start | bytes 3145736 | tf_op jit(solution)/shard_map/ppermute | solution.py:376
  68.4 4.0 copy-start
  115.6 4.3 collective-permute-start.6
  117.3 4.0 collective-permute-start.7
  117.4 24.6 %collective-permute-start.8 = (bf16[2,1024,256]{2,1,0:T(8,128)(2,1)}, bf16[2,1024,256]{2,1,0:T(8,128)(2,1)S(1)}, u32[]{:S(2)}, u32[]{:S(2)}) collective-permute-start(bf16[2,1024,256]{2,1,0:T(8,128)(2,1)} %collective-permute-done.refs_4_), channel_id=1, source_target_pairs={{0,16},{16,0},{1,17},{17,1},{2,18},{18,2},{3,19},{19,3},{4,20},{20... | collective-permute-start | bytes 3145736 | tf_op jit(solution)/shard_map/ppermute | solution.py:381
  117.7 26.4 %collective-permute-start.9 = (bf16[2,1024,256]{2,1,0:T(8,128)(2,1)}, bf16[2,1024,256]{2,1,0:T(8,128)(2,1)S(1)}, u32[]{:S(2)}, u32[]{:S(2)}) collective-permute-start(bf16[2,1024,256]{2,1,0:T(8,128)(2,1)} %collective-permute-done.refs_4_), channel_id=1, source_target_pairs={{0,1},{1,0},{2,3},{3,2},{4,5},{5,4},{6,7},{7,6},{8,9},{9,8},{10,11... | collective-permute-start | bytes 3145736 | tf_op jit(solution)/shard_map/ppermute | solution.py:376
  118.4 46.1 %collective-permute-start.11 = (bf16[2,1024,256]{2,1,0:T(8,128)(2,1)}, bf16[2,1024,256]{2,1,0:T(8,128)(2,1)}, u32[]{:S(2)}, u32[]{:S(2)}) collective-permute-start(bf16[2,1024,256]{2,1,0:T(8,128)(2,1)} %collective-permute-done.1.refs_8_), channel_id=1, source_target_pairs={{0,16},{16,0},{1,17},{17,1},{2,18},{18,2},{3,19},{19,3},{4,20},{20... | collective-permute-start | bytes 3145736 | tf_op jit(solution)/shard_map/ppermute | solution.py:381
  119.8 1.5 copy-start.8
  119.8 44.9 %collective-permute-start.12 = (bf16[2,1024,256]{2,1,0:T(8,128)(2,1)}, bf16[2,1024,256]{2,1,0:T(8,128)(2,1)}, u32[]{:S(2)}, u32[]{:S(2)}) collective-permute-start(bf16[2,1024,256]{2,1,0:T(8,128)(2,1)} %collective-permute-done.1.refs_8_), channel_id=1, source_target_pairs={{0,1},{1,0},{2,3},{3,2},{4,5},{5,4},{6,7},{7,6},{8,9},{9,8},{10,11... | collective-permute-start | bytes 3145736 | tf_op jit(solution)/shard_map/ppermute | solution.py:376
  121.3 1.0 copy-start.9
  121.3 65.6 %collective-permute-start.14 = (bf16[2,1024,256]{2,1,0:T(8,128)(2,1)}, bf16[2,1024,256]{2,1,0:T(8,128)(2,1)S(1)}, u32[]{:S(2)}, u32[]{:S(2)}) collective-permute-start(bf16[2,1024,256]{2,1,0:T(8,128)(2,1)} %collective-permute-done.2.refs_12_), channel_id=1, source_target_pairs={{0,16},{16,0},{1,17},{17,1},{2,18},{18,2},{3,19},{19,3},{4,20},{20... | collective-permute-start | bytes 3145736 | tf_op jit(solution)/shard_map/ppermute | solution.py:381
  142.0 47.6 %copy-start.10 = (bf16[2,1024,256]{2,1,0:T(8,128)(2,1)}, bf16[2,1024,256]{2,1,0:T(8,128)(2,1)S(1)}, u32[]{:S(2)}) copy-start(bf16[2,1024,256]{2,1,0:T(8,128)(2,1)S(1)} %collective-permute-done.8.refs_5_) | copy-start | bytes 3145732
  142.0 45.2 %collective-permute-start.15 = (bf16[2,1024,256]{2,1,0:T(8,128)(2,1)}, bf16[2,1024,256]{2,1,0:T(8,128)(2,1)}, u32[]{:S(2)}, u32[]{:S(2)}) collective-permute-start(bf16[2,1024,256]{2,1,0:T(8,128)(2,1)} %collective-permute-done.2.refs_12_), channel_id=1, source_target_pairs={{0,1},{1,0},{2,3},{3,2},{4,5},{5,4},{6,7},{7,6},{8,9},{9,8},{10,11... | collective-permute-start | bytes 3145736 | tf_op jit(solution)/shard_map/ppermute | solution.py:376
  144.1 173.9 %copy-start.11 = (bf16[2,1024,256]{2,1,0:T(8,128)(2,1)}, bf16[2,1024,256]{2,1,0:T(8,128)(2,1)S(1)}, u32[]{:S(2)}) copy-start(bf16[2,1024,256]{2,1,0:T(8,128)(2,1)S(1)} %collective-permute-done.9.refs_6_) | copy-start | bytes 3145732
  144.1 45.4 %collective-permute-start.10 = (bf16[2,1024,256]{2,1,0:T(8,128)(2,1)S(1)}, bf16[2,1024,256]{2,1,0:T(8,128)(2,1)}, u32[]{:S(2)}, u32[]{:S(2)}) collective-permute-start(bf16[2,1024,256]{2,1,0:T(8,128)(2,1)S(1)} %collective-permute-done.8.refs_5_), channel_id=1, source_target_pairs={{0,1},{1,0},{2,3},{3,2},{4,5},{5,4},{6,7},{7,6},{8,9},{9,8},{10,11... | collective-permute-start | bytes 3145736 | tf_op jit(solution)/shard_map/ppermute | solution.py:376
  144.3 173.7 %copy-start.7 = (s32[16]{0:T(128)}, s32[16]{0:T(128)S(1)}, u32[]{:S(2)}) copy-start(s32[16]{0:T(128)S(1)} %stack.89.src_ref) | copy-start | bytes 196
  164.5 77.0 %collective-permute-start.17 = (bf16[2,1024,256]{2,1,0:T(8,128)(2,1)}, bf16[2,1024,256]{2,1,0:T(8,128)(2,1)}, u32[]{:S(2)}, u32[]{:S(2)}) collective-permute-start(bf16[2,1024,256]{2,1,0:T(8,128)(2,1)} %collective-permute-done.3.refs_16_), channel_id=1, source_target_pairs={{0,16},{16,0},{1,17},{17,1},{2,18},{18,2},{3,19},{19,3},{4,20},{20... | collective-permute-start | bytes 3145736 | tf_op jit(solution)/shard_map/ppermute | solution.py:381
  164.7 78.0 %collective-permute-start.18 = (bf16[2,1024,256]{2,1,0:T(8,128)(2,1)}, bf16[2,1024,256]{2,1,0:T(8,128)(2,1)}, u32[]{:S(2)}, u32[]{:S(2)}) collective-permute-start(bf16[2,1024,256]{2,1,0:T(8,128)(2,1)} %collective-permute-done.3.refs_16_), channel_id=1, source_target_pairs={{0,1},{1,0},{2,3},{3,2},{4,5},{5,4},{6,7},{7,6},{8,9},{9,8},{10,11... | collective-permute-start | bytes 3145736 | tf_op jit(solution)/shard_map/ppermute | solution.py:376
  187.0 131.1 %copy-start.12 = (bf16[2,1024,256]{2,1,0:T(8,128)(2,1)}, bf16[2,1024,256]{2,1,0:T(8,128)(2,1)S(1)}, u32[]{:S(2)}) copy-start(bf16[2,1024,256]{2,1,0:T(8,128)(2,1)S(1)} %collective-permute-done.14.refs_13_) | copy-start | bytes 3145732
  187.0 56.6 %collective-permute-start.26 = (bf16[2,1024,256]{2,1,0:T(8,128)(2,1)}, bf16[2,1024,256]{2,1,0:T(8,128)(2,1)}, u32[]{:S(2)}, u32[]{:S(2)}) collective-permute-start(bf16[2,1024,256]{2,1,0:T(8,128)(2,1)} %collective-permute-done.5.refs_24_), channel_id=1, source_target_pairs={{0,2},{1,3},{2,0},{3,1},{4,6},{5,7},{6,4},{7,5},{8,10},{9,11},{10,... | collective-permute-start | bytes 3145736 | tf_op jit(solution)/shard_map/ppermute | solution.py:376
  187.2 54.0 %collective-permute-start.13 = (bf16[2,1024,256]{2,1,0:T(8,128)(2,1)}, bf16[2,1024,256]{2,1,0:T(8,128)(2,1)}, u32[]{:S(2)}, u32[]{:S(2)}) collective-permute-start(bf16[2,1024,256]{2,1,0:T(8,128)(2,1)} %collective-permute-done.11.refs_9_), channel_id=1, source_target_pairs={{0,1},{1,0},{2,3},{3,2},{4,5},{5,4},{6,7},{7,6},{8,9},{9,8},{10,11... | collective-permute-start | bytes 3145736 | tf_op jit(solution)/shard_map/ppermute | solution.py:376
  189.5 52.0 %collective-permute-start.16 = (bf16[2,1024,256]{2,1,0:T(8,128)(2,1)S(1)}, bf16[2,1024,256]{2,1,0:T(8,128)(2,1)}, u32[]{:S(2)}, u32[]{:S(2)}) collective-permute-start(bf16[2,1024,256]{2,1,0:T(8,128)(2,1)S(1)} %collective-permute-done.14.refs_13_), channel_id=1, source_target_pairs={{0,1},{1,0},{2,3},{3,2},{4,5},{5,4},{6,7},{7,6},{8,9},{9,8},{10,11... | collective-permute-start | bytes 3145736 | tf_op jit(solution)/shard_map/ppermute | solution.py:376
  190.6 50.4 %all-to-all-start = ((f32[16,3,10,128]{3,1,2,0:T(4,128)}), f32[16,3,10,128]{3,1,2,0:T(4,128)S(1)}, u32[]{:S(2)}, u32[]{:S(2)}) async-start(f32[16,3,10,128]{3,1,2,0:T(4,128)} %copy.88), calls=%async_computation | async-start | bytes 655360 | tf_op jit(solution)/shard_map/all_to_all | solution.py:421
  241.2 25.5 %collective-permute-start.20 = (bf16[2,1024,256]{2,1,0:T(8,128)(2,1)}, bf16[2,1024,256]{2,1,0:T(8,128)(2,1)}, u32[]{:S(2)}, u32[]{:S(2)}) collective-permute-start(bf16[2,1024,256]{2,1,0:T(8,128)(2,1)} %collective-permute-done.4.refs_20_), channel_id=1, source_target_pairs={{0,16},{16,0},{1,17},{17,1},{2,18},{18,2},{3,19},{19,3},{4,20},{20... | collective-permute-start | bytes 3145736 | tf_op jit(solution)/shard_map/ppermute | solution.py:381
  241.5 25.7 %collective-permute-start.21 = (bf16[2,1024,256]{2,1,0:T(8,128)(2,1)}, bf16[2,1024,256]{2,1,0:T(8,128)(2,1)}, u32[]{:S(2)}, u32[]{:S(2)}) collective-permute-start(bf16[2,1024,256]{2,1,0:T(8,128)(2,1)} %collective-permute-done.4.refs_20_), channel_id=1, source_target_pairs={{0,1},{1,0},{2,3},{3,2},{4,5},{5,4},{6,7},{7,6},{8,9},{9,8},{10,11... | collective-permute-start | bytes 3145736 | tf_op jit(solution)/shard_map/ppermute | solution.py:376
  241.5 47.6 %collective-permute-start.23 = (bf16[2,1024,256]{2,1,0:T(8,128)(2,1)}, bf16[2,1024,256]{2,1,0:T(8,128)(2,1)}, u32[]{:S(2)}, u32[]{:S(2)}) collective-permute-start(bf16[2,1024,256]{2,1,0:T(8,128)(2,1)} %collective-permute-done.5.refs_24_), channel_id=1, source_target_pairs={{0,16},{16,0},{1,17},{17,1},{2,18},{18,2},{3,19},{19,3},{4,20},{20... | collective-permute-start | bytes 3145736 | tf_op jit(solution)/shard_map/ppermute | solution.py:381
  242.8 46.9 %collective-permute-start.24 = (bf16[2,1024,256]{2,1,0:T(8,128)(2,1)}, bf16[2,1024,256]{2,1,0:T(8,128)(2,1)}, u32[]{:S(2)}, u32[]{:S(2)}) collective-permute-start(bf16[2,1024,256]{2,1,0:T(8,128)(2,1)} %collective-permute-done.5.refs_24_), channel_id=1, source_target_pairs={{0,1},{1,0},{2,3},{3,2},{4,5},{5,4},{6,7},{7,6},{8,9},{9,8},{10,11... | collective-permute-start | bytes 3145736 | tf_op jit(solution)/shard_map/ppermute | solution.py:376
  243.5 68.1 %collective-permute-start.27 = (bf16[2,1024,256]{2,1,0:T(8,128)(2,1)}, bf16[2,1024,256]{2,1,0:T(8,128)(2,1)}, u32[]{:S(2)}, u32[]{:S(2)}) collective-permute-start(bf16[2,1024,256]{2,1,0:T(8,128)(2,1)} %collective-permute-done.26.refs_28_), channel_id=1, source_target_pairs={{0,16},{16,0},{1,17},{17,1},{2,18},{18,2},{3,19},{19,3},{4,20},{20... | collective-permute-start | bytes 3145736 | tf_op jit(solution)/shard_map/ppermute | solution.py:381
  266.6 54.0 %collective-permute-start.28 = (bf16[2,1024,256]{2,1,0:T(8,128)(2,1)}, bf16[2,1024,256]{2,1,0:T(8,128)(2,1)}, u32[]{:S(2)}, u32[]{:S(2)}) collective-permute-start(bf16[2,1024,256]{2,1,0:T(8,128)(2,1)} %collective-permute-done.26.refs_28_), channel_id=1, source_target_pairs={{0,1},{1,0},{2,3},{3,2},{4,5},{5,4},{6,7},{7,6},{8,9},{9,8},{10,11... | collective-permute-start | bytes 3145736 | tf_op jit(solution)/shard_map/ppermute | solution.py:376
  267.2 53.4 %collective-permute-start.19 = (bf16[2,1024,256]{2,1,0:T(8,128)(2,1)}, bf16[2,1024,256]{2,1,0:T(8,128)(2,1)}, u32[]{:S(2)}, u32[]{:S(2)}) collective-permute-start(bf16[2,1024,256]{2,1,0:T(8,128)(2,1)} %collective-permute-done.17.refs_17_), channel_id=1, source_target_pairs={{0,1},{1,0},{2,3},{3,2},{4,5},{5,4},{6,7},{7,6},{8,9},{9,8},{10,11... | collective-permute-start | bytes 3145736 | tf_op jit(solution)/shard_map/ppermute | solution.py:376
  289.1 31.6 %collective-permute-start.22 = (bf16[2,1024,256]{2,1,0:T(8,128)(2,1)}, bf16[2,1024,256]{2,1,0:T(8,128)(2,1)}, u32[]{:S(2)}, u32[]{:S(2)}) collective-permute-start(bf16[2,1024,256]{2,1,0:T(8,128)(2,1)} %collective-permute-done.20.refs_21_), channel_id=1, source_target_pairs={{0,1},{1,0},{2,3},{3,2},{4,5},{5,4},{6,7},{7,6},{8,9},{9,8},{10,11... | collective-permute-start | bytes 3145736 | tf_op jit(solution)/shard_map/ppermute | solution.py:376
  289.7 31.0 %collective-permute-start.25 = (bf16[2,1024,256]{2,1,0:T(8,128)(2,1)}, bf16[2,1024,256]{2,1,0:T(8,128)(2,1)}, u32[]{:S(2)}, u32[]{:S(2)}) collective-permute-start(bf16[2,1024,256]{2,1,0:T(8,128)(2,1)} %collective-permute-done.23.refs_25_), channel_id=1, source_target_pairs={{0,1},{1,0},{2,3},{3,2},{4,5},{5,4},{6,7},{7,6},{8,9},{9,8},{10,11... | collective-permute-start | bytes 3145736 | tf_op jit(solution)/shard_map/ppermute | solution.py:376
  311.6 9.1 %collective-permute-start.29 = (bf16[2,1024,256]{2,1,0:T(8,128)(2,1)}, bf16[2,1024,256]{2,1,0:T(8,128)(2,1)}, u32[]{:S(2)}, u32[]{:S(2)}) collective-permute-start(bf16[2,1024,256]{2,1,0:T(8,128)(2,1)} %collective-permute-done.27.refs_29_), channel_id=1, source_target_pairs={{0,1},{1,0},{2,3},{3,2},{4,5},{5,4},{6,7},{7,6},{8,9},{9,8},{10,11... | collective-permute-start | bytes 3145736 | tf_op jit(solution)/shard_map/ppermute | solution.py:376
Sparse Core Ops, SparseCore 0:
  115.7 193.2 all-gather.1

commit v4 on v3

--- a/solution.py
+++ b/solution.py
@@ -15,7 +15,7 @@
 TILE = 128
 PICK_TILE = 256
 TOKEN_UNROLL = 2
-OWNER_TILE = 256
+OWNER_TILE = 512
 MOVE_ROWS = 64
 ALIGN = 16
 LANES = 128
@@ -55,8 +55,9 @@
     return jnp.where(tok == cols, 1.0, 0.0).astype(jnp.bfloat16)
 
 
-def pick_kernel(n_ref, meta_ref, x_ref, dy_ref, rows_ref, drow_ref):
-    used = n_ref[pl.program_id(0)]
+def pick_kernel(first, n_ref, meta_ref, x_ref, dy_ref, *refs):
+    rows_ref, drow_ref = refs[-2:]
+    used = n_ref[first + pl.program_id(0)]
 
     def tile(i, carry):
         at = pl.ds(pl.multiple_of(i * PICK_TILE, PICK_TILE), PICK_TILE)
@@ -68,25 +69,26 @@
     lax.fori_loop(0, (used + PICK_TILE - 1) // PICK_TILE, tile, 0)
 
 
-def pick_pass(used, meta, x, dy):
+def pick_pass(used, meta, x, dy, first, count, into=()):
     n_tokens, d = x.shape
-    dests = used.shape[0]
-    block_rows = meta.shape[0] // dests
+    block_rows = meta.shape[0] // used.shape[0]
     whole = lambda e, *_: (0, 0)
-    row = lambda e, *_: (e, 0)
+    row = lambda e, *_: (first + e, 0)
     out = jax.ShapeDtypeStruct((meta.shape[0], d), jnp.bfloat16)
     return pl.pallas_call(
-        pick_kernel,
+        functools.partial(pick_kernel, first),
         out_shape=(out, out),
         grid_spec=pltpu.PrefetchScalarGridSpec(
-            num_scalar_prefetch=1, grid=(dests,),
+            num_scalar_prefetch=1, grid=(count,),
             in_specs=[pl.BlockSpec((block_rows, 2), row),
-                      pl.BlockSpec((n_tokens, d), whole), pl.BlockSpec((n_tokens, d), whole)],
+                      pl.BlockSpec((n_tokens, d), whole), pl.BlockSpec((n_tokens, d), whole),
+                      *[pl.BlockSpec(memory_space=pl.ANY) for _ in into]],
             out_specs=[pl.BlockSpec((block_rows, d), row), pl.BlockSpec((block_rows, d), row)]),
         compiler_params=pltpu.CompilerParams(dimension_semantics=("arbitrary",), vmem_limit_bytes=VMEM_BYTES // 2),
-        cost_estimate=pl.CostEstimate(flops=20_000_000_000, bytes_accessed=50_000_000, transcendentals=0),
+        input_output_aliases={4 + k: k for k in range(len(into))},
+        cost_estimate=pl.CostEstimate(flops=10_000_000_000, bytes_accessed=25_000_000, transcendentals=0),
         name="pick_pass",
-    )(used, meta, x, dy)
+    )(used, meta, x, dy, *into)
 
 
 def out_product(act, w):
@@ -329,7 +331,7 @@
     return a, b, lax.reduce_precision(v - a - b, 8, 7)
 
 
-def route(expert_idx, gate, num_experts, groups, list_rows):
+def route(expert_idx, gate, num_experts, groups, list_rows, hold):
     n_tokens, top_k = expert_idx.shape
     n_pairs = n_tokens * top_k
     local_experts = num_experts // groups
@@ -355,9 +357,10 @@
     token = jnp.arange(n_pairs, dtype=jnp.int32) // top_k
     parts = [(token // 32).astype(jnp.float32), (token % 32).astype(jnp.float32), *split3(gate.reshape(n_pairs))]
     vals = jnp.concatenate([jnp.where(lo, v[:, None], 0.0).astype(jnp.bfloat16) for v in parts], axis=1)
+    vals, *hold = lax.optimization_barrier((vals, *hold))
     lists = lax.dot_general(hi, vals, (((0,), (0,)), ((), ())), preferred_element_type=jnp.float32)
     t_hi, t_lo, g1, g2, g3 = (lists[:, k * LANES:(k + 1) * LANES] for k in range(5))
-    return flat, hot, rank, counts, padded, local_start, 32.0 * t_hi + t_lo, g1 + g2 + g3
+    return flat, hot, rank, counts, padded, local_start, 32.0 * t_hi + t_lo, g1 + g2 + g3, hold
 
 
 def columns(tokens, gates):
@@ -405,36 +408,42 @@
         other = lax.dynamic_slice_in_dim(w_own, (1 - my_data) * half, half, axis=0)
         z_by, y_swap, c_swap, x_swap = mesh_moves(groups // 4, 2)
         near, z1, z3 = y_swap(ring), z_by[1](ring), z_by[3](ring)
-        _, hot, rank, counts, padded, local_start, tok_list, gate_list = route(
-            expert_idx, gate_weight, num_experts, groups, list_rows)
-        near, z1, z3, ring_late, tok_list, gate_list = lax.optimization_barrier((near, z1, z3, ring, tok_list, gate_list))
+        flat, hot, rank, counts, padded, local_start, tok_list, gate_list, (near, ring_late) = route(
+            expert_idx, gate_weight, num_experts, groups, list_rows, (near, ring))
         z2 = z_by[2](ring_late)
         near_x = x_swap(near)
+
+        meta = columns(tok_list, gate_list)
+        used = jnp.sum(padded.reshape(groups, local_experts), axis=1)
+        z1, z3, used, meta = lax.optimization_barrier((z1, z3, used, meta))
+        z1_y = y_swap(z1)
+        z3_y = y_swap(z3)
         z1_x = x_swap(z1)
         z3_x = x_swap(z3)
-        z1_y, z3_y = y_swap(z1), y_swap(z3)
+        z2_y = y_swap(z2)
+        z2_x = x_swap(z2)
         xy = jnp.concatenate([x_in, grad_y], axis=0)
-
+        z1_y, z3_y, xy = lax.optimization_barrier((z1_y, z3_y, xy))
+        xy_all = lax.all_gather(xy, 'expert', axis=0, tiled=True)
+        z1_yx = x_swap(z1_y)
+        z3_yx = x_swap(z3_y)
+        z2_y, used = lax.optimization_barrier((z2_y, used))
+        z2_yx = x_swap(z2_y)
+        rows, drow = pick_pass(used, meta, x_in, grad_y, 0, groups)
         count_plane = jnp.zeros((list_rows // LANES, LANES), jnp.float32).at[0, 0:num_experts].set(counts.astype(jnp.float32))
         lists = jnp.stack([tok_list.reshape(groups, -1, LANES), gate_list.reshape(groups, -1, LANES),
                            jnp.broadcast_to(count_plane, (groups, *count_plane.shape))], axis=1)
+        lists, _ = lax.optimization_barrier((lists, rows))
         lists = lax.all_to_all(lists, 'expert', 0, 0, tiled=True)
         counts_all = lists[:, 2, 0, 0:num_experts].astype(jnp.int32)
         before = jnp.cumsum(counts_all, axis=0) - counts_all
         kept_all = jnp.clip(capacity - before, 0, counts_all)
         kept_mine = lax.dynamic_index_in_dim(kept_all, me, 0, keepdims=False)
 
-        meta = columns(tok_list, gate_list)
-        used = jnp.sum(padded.reshape(groups, local_experts), axis=1)
-        rows, drow = pick_pass(used, meta, x_in, grad_y)
-        z1_y, z3_y, z2, rows, drow = lax.optimization_barrier((z1_y, z3_y, z2, rows, drow))
-        z2_y = y_swap(z2)
-        xy, _ = lax.optimization_barrier((xy, rows))
-        xy_all = lax.all_gather(xy, 'expert', axis=0, tiled=True)
         halves, where = [], []
         for at, v, u in [((0, 0), ring, other), ((0, 1), near, near_x), ((1, 0), z1, z1_x), ((3, 0), z3, z3_x),
-                         ((1, 1), z1_y, x_swap(z1_y)), ((3, 1), z3_y, x_swap(z3_y)),
-                         ((2, 0), z2, x_swap(z2)), ((2, 1), z2_y, x_swap(z2_y))]:
+                         ((1, 1), z1_y, z1_yx), ((3, 1), z3_y, z3_yx),
+                         ((2, 0), z2, z2_x), ((2, 1), z2_y, z2_yx)]:
             halves += [(v, u), (c_swap(v), c_swap(u))]
             where += [(*at, 0), (*at, 1)]
 

time: 474 us -> 524 us (1.11)
  the two profiles are of different devices: /device:TPU:3 before, /device:TPU:1 now
where the time goes in v4:
time: 524 us
  waiting for transfers between devices  233 us (44%)
  Pallas kernels  174 us (33%)
  starting transfers between devices  50.4 us (10%)
  other arithmetic  24.9 us (5%)
  local copies, waits for them, and re-layouts  23.3 us (4%)
  between operations  14.5 us (3%)
    ppermute x23, waiting for transfers between devices, along(): return lambda v: lax.ppermute(v, 'expert', pairs)  159 us
    pallas_call x1, Pallas kernels, token_pass(): pl.pallas_call(functools.partial(token_kernel, zero_row, top_k, slots), o...  72.6 us
    pallas_call x1, Pallas kernels, owner_pass(): pl.pallas_call(owner_kernel, out_shape=(jax.ShapeDtypeStruct(w1.shape, jn...  64.9 us
    ppermute x7, waiting for transfers between devices, mesh_moves(): lax.ppermute(v, 'data', [(0, 1), (1, 0)])  59.4 us
    ppermute x23, starting transfers between devices, along(): return lambda v: lax.ppermute(v, 'expert', pairs)  37.8 us
    pallas_call x1, Pallas kernels, pick_pass(): pl.pallas_call(functools.partial(pick_kernel, first), out_shape=(out, out...  36.4 us
    all_to_all x1, waiting for transfers between devices, device_pass(): lists = lax.all_to_all(lists, 'expert', 0, 0, tiled=True)  15.3 us
    unnamed x5, other arithmetic  13.3 us
  transfers between devices with their start and end apart: 32, of which 9 were waited for; matrix products, arithmetic and copies ran while one was open for 8% of the time, Pallas kernels for 21%

profile of v4, /device:TPU:1, one launch (start us, length us, event | category | flops | bytes accessed | tf_op | source)
XLA Modules:
  0.0 523.7 jit_solution(4682705898143199862)
XLA Ops:
  7.2 1.3 fusion.54
  8.5 1.4 pad_maximum_fusion
  9.9 1.5 constant_dynamic-slice_fusion.2
  11.3 2.1 collective-permute-start
  13.4 1.3 collective-permute-start.3
  14.7 2.0 collective-permute-start.4
  18.6 0.9 fusion.2
  20.5 2.7 fusion.3
  23.2 3.5 fusion.4
  26.8 3.5 fusion.5
  30.3 3.5 fusion.6
  33.9 3.8 fusion.7
  37.7 2.4 fusion
  40.3 21.7 %collective-permute-done.4.refs_12_ = bf16[2,1024,256]{2,1,0:T(8,128)(2,1)} collective-permute-done((bf16[2,1024,256]{2,1,0:T(8,128)(2,1)}, bf16[2,1024,256]{2,1,0:T(8,128)(2,1)}, u32[]{:S(2)}, u32[]{:S(2)}) %collective-permute-start.4) | collective-permute-done | bytes 1048608 | tf_op jit(solution)/shard_map/ppermute | solution.py:379
  62.2 1.2 collective-permute-start.17
  63.4 1.5 pad_maximum_fusion.1
  65.0 21.0 %collective-permute-done.16.refs_16_ = bf16[2,1024,256]{2,1,0:T(8,128)(2,1)} collective-permute-done((bf16[2,1024,256]{2,1,0:T(8,128)(2,1)}, bf16[2,1024,256]{2,1,0:T(8,128)(2,1)}, u32[]{:S(2)}, u32[]{:S(2)}) %collective-permute-start.16) | collective-permute-done | bytes 1048608 | tf_op jit(solution)/shard_map/ppermute | solution.py:379
  85.9 22.5 %collective-permute-done.17.refs_20_ = bf16[2,1024,256]{2,1,0:T(8,128)(2,1)} collective-permute-done((bf16[2,1024,256]{2,1,0:T(8,128)(2,1)}, bf16[2,1024,256]{2,1,0:T(8,128)(2,1)}, u32[]{:S(2)}, u32[]{:S(2)}) %collective-permute-start.17) | collective-permute-done | bytes 1048608 | tf_op jit(solution)/shard_map/ppermute | solution.py:379
  108.5 2.7 collective-permute-start.5
  111.2 1.2 collective-permute-start.7
  112.4 61.8 %collective-permute-done.1.refs_24_ = bf16[2,1024,256]{2,1,0:T(8,128)(2,1)} collective-permute-done((bf16[2,1024,256]{2,1,0:T(8,128)(2,1)}, bf16[2,1024,256]{2,1,0:T(8,128)(2,1)}, u32[]{:S(2)}, u32[]{:S(2)}) %collective-permute-start.1) | collective-permute-done | bytes 1048608 | tf_op jit(solution)/shard_map/ppermute | solution.py:379
  174.4 6.3 %collective-permute-start.8 = (bf16[2,1024,256]{2,1,0:T(8,128)(2,1)}, bf16[2,1024,256]{2,1,0:T(8,128)(2,1)}, u32[]{:S(2)}, u32[]{:S(2)}) collective-permute-start(bf16[2,1024,256]{2,1,0:T(8,128)(2,1)} %collective-permute-done.refs_4_), channel_id=1, source_target_pairs={{0,1},{1,0},{2,3},{3,2},{4,5},{5,4},{6,7},{7,6},{8,9},{9,8},{10,11... | collective-permute-start | bytes 3145736 | tf_op jit(solution)/shard_map/ppermute | solution.py:379
  180.7 1.2 collective-permute-start.10
  182.5 31.7 %collective-permute-done.2.refs_28_ = bf16[2,1024,256]{2,1,0:T(8,128)(2,1)} collective-permute-done((bf16[2,1024,256]{2,1,0:T(8,128)(2,1)}, bf16[2,1024,256]{2,1,0:T(8,128)(2,1)}, u32[]{:S(2)}, u32[]{:S(2)}) %collective-permute-start.2) | collective-permute-done | bytes 1048608 | tf_op jit(solution)/shard_map/ppermute | solution.py:379
  214.2 11.1 %collective-permute-start.14 = (bf16[2,1024,256]{2,1,0:T(8,128)(2,1)}, bf16[2,1024,256]{2,1,0:T(8,128)(2,1)}, u32[]{:S(2)}, u32[]{:S(2)}) collective-permute-start(bf16[2,1024,256]{2,1,0:T(8,128)(2,1)} %collective-permute-done.4.refs_12_), channel_id=1, source_target_pairs={{0,1},{1,0},{2,3},{3,2},{4,5},{5,4},{6,7},{7,6},{8,9},{9,8},{10,11... | collective-permute-start | bytes 3145736 | tf_op jit(solution)/shard_map/ppermute | solution.py:379
  225.4 5.4 %copy.88.meta_ref = f32[20480,2]{1,0:T(8,128)} copy(f32[20480,2]{0,1:T(2,128)S(1)} %pad_maximum_fusion.3) | data formatting | bytes 327680 | tf_op jit(solution)/shard_map/optimization_barrier | solution.py:418
  230.9 1.3 collective-permute-start.18
  233.3 4.1 copy-done
  237.4 36.4 %pick_pass.1 = (bf16[20480,512]{1,0:T(8,128)(2,1)}, bf16[20480,512]{1,0:T(8,128)(2,1)}) custom-call(s32[16]{0:T(128)S(1)} %get-tuple-element.40.n_ref, f32[20480,2]{1,0:T(8,128)S(1)} %copy-done, bf16[1024,512]{1,0:T(8,128)(2,1)S(1)} %copy-done.1, bf16[1024,512]{1,0:T(8,128)(2,1)S(1)} %copy-done.2), custom_call_target="tpu_custom_call" | custom-call | flops 10000000000 | bytes 25000000 | tf_op jit(solution)/shard_map/pick_pass/pallas_call | solution.py:78
  273.8 0.9 copy.89
  274.7 7.0 %all-to-all-start = ((f32[16,3,10,128]{3,1,2,0:T(4,128)}), f32[16,3,10,128]{3,1,2,0:T(4,128)S(1)}, u32[]{:S(2)}, u32[]{:S(2)}) async-start(f32[16,3,10,128]{3,1,2,0:T(4,128)} %copy.89), calls=%async_computation | async-start | bytes 655360 | tf_op jit(solution)/shard_map/all_to_all | solution.py:437
  282.4 15.3 %all-to-all-done = f32[16,3,10,128]{3,1,2,0:T(4,128)S(1)} async-done(((f32[16,3,10,128]{3,1,2,0:T(4,128)}), f32[16,3,10,128]{3,1,2,0:T(4,128)S(1)}, u32[]{:S(2)}, u32[]{:S(2)}) %all-to-all-start) | async-done | bytes 245792 | tf_op jit(solution)/shard_map/all_to_all | solution.py:437
  298.0 1.1 collective-permute-start.22
  299.1 1.4 collective-permute-start.24
  301.6 20.4 %collective-permute-done.21.refs_21_ = bf16[2,1024,256]{2,1,0:T(8,128)(2,1)S(1)} collective-permute-done((bf16[2,1024,256]{2,1,0:T(8,128)(2,1)}, bf16[2,1024,256]{2,1,0:T(8,128)(2,1)S(1)}, u32[]{:S(2)}, u32[]{:S(2)}) %collective-permute-start.21) | collective-permute-done | bytes 1048608 | tf_op jit(solution)/shard_map/ppermute | solution.py:384
  322.0 3.0 collective-permute-start.28
  325.1 19.5 %collective-permute-done.24.refs_25_ = bf16[2,1024,256]{2,1,0:T(8,128)(2,1)} collective-permute-done((bf16[2,1024,256]{2,1,0:T(8,128)(2,1)}, bf16[2,1024,256]{2,1,0:T(8,128)(2,1)}, u32[]{:S(2)}, u32[]{:S(2)}) %collective-permute-start.24) | collective-permute-done | bytes 1048608 | tf_op jit(solution)/shard_map/ppermute | solution.py:384
  344.6 3.0 collective-permute-start.23
  347.6 19.5 %collective-permute-done.27.refs_29_ = bf16[2,1024,256]{2,1,0:T(8,128)(2,1)} collective-permute-done((bf16[2,1024,256]{2,1,0:T(8,128)(2,1)}, bf16[2,1024,256]{2,1,0:T(8,128)(2,1)}, u32[]{:S(2)}, u32[]{:S(2)}) %collective-permute-start.27) | collective-permute-done | bytes 1048608 | tf_op jit(solution)/shard_map/ppermute | solution.py:384
  367.1 1.7 collective-permute-start.29
  369.3 5.5 %copy.100.meta_ref = f32[20480,2]{1,0:T(8,128)} copy(f32[20480,2]{0,1:T(2,128)S(1)} %pad_maximum_fusion.4) | data formatting | bytes 327680 | tf_op jit(solution)/shard_map/stack | solution.py:367
  374.8 0.6 pad_add_fusion.1.sc_ref
  375.6 0.6 pad_add_fusion.sc_ref
  376.2 0.6 select_reduce_fusion.1
  376.8 0.6 add_select_fusion.6.pos_ref
  377.5 72.6 %token_pass.1 = (bf16[1024,512]{1,0:T(8,128)(2,1)}, bf16[1024,512]{1,0:T(8,128)(2,1)}, f32[1024,128]{1,0:T(8,128)}) custom-call(s32[3,64]{1,0:T(4,128)} %pad_add_fusion.sc_ref, s32[16]{0:T(128)} %copy-done.5, s32[8192]{0:T(1024)} %add_select_fusion.6.pos_ref, f32[20480,2]{1,0:T(8,128)} %copy.88.meta_ref, bf16[20480,512]{1,0:T(8,128)(2,1)} %get-tuple-element.42.rows_ref, ...), custom_call_target="tpu_custom_call" | custom-call | flops 40000000000 | bytes 80000000 | tf_op jit(solution)/shard_map/token_pass/pallas_call | solution.py:212
  450.1 1.8 copy.101
  451.9 64.9 %owner_pass.1 = (bf16[4,512,256]{2,1,0:T(8,128)(2,1)}, bf16[4,256,512]{2,1,0:T(8,128)(2,1)}) custom-call(s32[3,64]{1,0:T(4,128)} %pad_add_fusion.1.sc_ref, f32[20480,2]{1,0:T(8,128)} %copy.100.meta_ref, bf16[32768,512]{1,0:T(8,128)(2,1)} %all-gather.2.cloned.1.call-done.xy_ref, bf16[4,512,256]{2,1,0:T(8,128)(2,1)} %w1_ref.1, bf16[4,256,512]{2,1,0:T(8,128)(2,1)} %w2_ref.1), custom_call_target="tpu_custom_call" | custom-call | flops 60000002048 | bytes 50000000 | tf_op jit(solution)/shard_map/owner_pass/pallas_call | solution.py:307
  (120 shorter events, 8.0 us)
Async XLA Ops:
  7.2 444.7 %all-gather.2.cloned.1.call-start = ((), (), s32[]{:S(2)}) async-start(), calls=%async_computation.1 | async-start | bytes 35651584 | tf_op jit(solution)/shard_map/all_gather | solution.py:427
  8.5 8.3 %copy-start.3 = (s32[1024,8]{0,1:T(8,128)S(1)}, s32[1024,8]{0,1:T(8,128)}, u32[]{:S(2)}) copy-start(s32[1024,8]{0,1:T(8,128)} %param.9) | copy-start | bytes 98308
  9.9 9.7 %copy-start.4 = (f32[1024,8]{0,1:T(8,128)S(1)}, f32[1024,8]{0,1:T(8,128)}, u32[]{:S(2)}) copy-start(f32[1024,8]{0,1:T(8,128)} %param.10) | copy-start | bytes 98308
  11.3 26.3 %collective-permute-start = (bf16[2,1024,256]{2,1,0:T(8,128)(2,1)}, bf16[2,1024,256]{2,1,0:T(8,128)(2,1)}, u32[]{:S(2)}, u32[]{:S(2)}) collective-permute-start(bf16[2,1024,256]{2,1,0:T(8,128)(2,1)} %get-tuple-element.38.refs_0_), channel_id=1, source_target_pairs={{0,2},{1,3},{2,0},{3,1},{4,6},{5,7},{6,4},{7,5},{8,10},{9,11},{10,... | collective-permute-start | bytes 3145736 | tf_op jit(solution)/shard_map/ppermute | solution.py:379
  13.4 26.9 %collective-permute-start.3 = (bf16[2,1024,256]{2,1,0:T(8,128)(2,1)}, bf16[2,1024,256]{2,1,0:T(8,128)(2,1)}, u32[]{:S(2)}, u32[]{:S(2)}) collective-permute-start(bf16[2,1024,256]{2,1,0:T(8,128)(2,1)} %get-tuple-element.38.refs_0_), channel_id=1, source_target_pairs={{0,4},{1,5},{2,6},{3,7},{4,8},{5,9},{6,10},{7,11},{8,12},{9,13},{1... | collective-permute-start | bytes 3145736 | tf_op jit(solution)/shard_map/ppermute | solution.py:379
  14.7 47.3 %collective-permute-start.4 = (bf16[2,1024,256]{2,1,0:T(8,128)(2,1)}, bf16[2,1024,256]{2,1,0:T(8,128)(2,1)}, u32[]{:S(2)}, u32[]{:S(2)}) collective-permute-start(bf16[2,1024,256]{2,1,0:T(8,128)(2,1)} %get-tuple-element.38.refs_0_), channel_id=1, source_target_pairs={{0,12},{1,13},{2,14},{3,15},{4,0},{5,1},{6,2},{7,3},{8,4},{9,5},{1... | collective-permute-start | bytes 3145736 | tf_op jit(solution)/shard_map/ppermute | solution.py:379
  37.6 25.8 %copy-start.1 = (bf16[1024,512]{1,0:T(8,128)(2,1)S(1)}, bf16[1024,512]{1,0:T(8,128)(2,1)}, u32[]{:S(2)}) copy-start(bf16[1024,512]{1,0:T(8,128)(2,1)} %x_ref.3) | copy-start | bytes 3145732
  37.6 25.8 %copy-start.2 = (bf16[1024,512]{1,0:T(8,128)(2,1)S(1)}, bf16[1024,512]{1,0:T(8,128)(2,1)}, u32[]{:S(2)}) copy-start(bf16[1024,512]{1,0:T(8,128)(2,1)} %dy_ref.3) | copy-start | bytes 3145732
  62.0 23.9 %collective-permute-start.16 = (bf16[2,1024,256]{2,1,0:T(8,128)(2,1)}, bf16[2,1024,256]{2,1,0:T(8,128)(2,1)}, u32[]{:S(2)}, u32[]{:S(2)}) collective-permute-start(bf16[2,1024,256]{2,1,0:T(8,128)(2,1)} %collective-permute-done.3.refs_8_), channel_id=1, source_target_pairs={{0,2},{1,3},{2,0},{3,1},{4,6},{5,7},{6,4},{7,5},{8,10},{9,11},{10,... | collective-permute-start | bytes 3145736 | tf_op jit(solution)/shard_map/ppermute | solution.py:379
  62.2 46.2 %collective-permute-start.17 = (bf16[2,1024,256]{2,1,0:T(8,128)(2,1)}, bf16[2,1024,256]{2,1,0:T(8,128)(2,1)}, u32[]{:S(2)}, u32[]{:S(2)}) collective-permute-start(bf16[2,1024,256]{2,1,0:T(8,128)(2,1)} %collective-permute-done.4.refs_12_), channel_id=1, source_target_pairs={{0,2},{1,3},{2,0},{3,1},{4,6},{5,7},{6,4},{7,5},{8,10},{9,11},{10,... | collective-permute-start | bytes 3145736 | tf_op jit(solution)/shard_map/ppermute | solution.py:379
  108.4 65.7 %collective-permute-start.1 = (bf16[2,1024,256]{2,1,0:T(8,128)(2,1)}, bf16[2,1024,256]{2,1,0:T(8,128)(2,1)}, u32[]{:S(2)}, u32[]{:S(2)}) collective-permute-start(bf16[2,1024,256]{2,1,0:T(8,128)(2,1)} %get-tuple-element.38.refs_0_), channel_id=1, source_target_pairs={{0,8},{1,9},{2,10},{3,11},{4,12},{5,13},{6,14},{7,15},{8,0},{9,1},... | collective-permute-start | bytes 3145736 | tf_op jit(solution)/shard_map/ppermute | solution.py:379
  108.5 72.2 %collective-permute-start.5 = (bf16[2,1024,256]{2,1,0:T(8,128)(2,1)}, bf16[2,1024,256]{2,1,0:T(8,128)(2,1)}, u32[]{:S(2)}, u32[]{:S(2)}) collective-permute-start(bf16[2,1024,256]{2,1,0:T(8,128)(2,1)} %get-tuple-element.38.refs_0_), channel_id=1, source_target_pairs={{0,1},{1,0},{2,3},{3,2},{4,5},{5,4},{6,7},{7,6},{8,9},{9,8},{10,11... | collective-permute-start | bytes 3145736 | tf_op jit(solution)/shard_map/ppermute | solution.py:379
  111.2 70.8 %collective-permute-start.6 = (bf16[2,1024,256]{2,1,0:T(8,128)(2,1)}, bf16[2,1024,256]{2,1,0:T(8,128)(2,1)}, u32[]{:S(2)}, u32[]{:S(2)}) collective-permute-start(bf16[2,1024,256]{2,1,0:T(8,128)(2,1)} %get-tuple-element.93.refs_1_), channel_id=1, source_target_pairs={{0,1},{1,0},{2,3},{3,2},{4,5},{5,4},{6,7},{7,6},{8,9},{9,8},{10,11... | collective-permute-start | bytes 3145736 | tf_op jit(solution)/shard_map/ppermute | solution.py:379
  111.2 71.0 %collective-permute-start.7 = (bf16[2,1024,256]{2,1,0:T(8,128)(2,1)}, bf16[2,1024,256]{2,1,0:T(8,128)(2,1)}, u32[]{:S(2)}, u32[]{:S(2)}) collective-permute-start(bf16[2,1024,256]{2,1,0:T(8,128)(2,1)} %collective-permute-done.refs_4_), channel_id=1, source_target_pairs={{0,16},{16,0},{1,17},{17,1},{2,18},{18,2},{3,19},{19,3},{4,20},{20... | collective-permute-start | bytes 3145736 | tf_op jit(solution)/shard_map/ppermute | solution.py:384
  174.1 40.0 %collective-permute-start.2 = (bf16[2,1024,256]{2,1,0:T(8,128)(2,1)}, bf16[2,1024,256]{2,1,0:T(8,128)(2,1)}, u32[]{:S(2)}, u32[]{:S(2)}) collective-permute-start(bf16[2,1024,256]{2,1,0:T(8,128)(2,1)} %collective-permute-done.1.refs_24_), channel_id=1, source_target_pairs={{0,2},{1,3},{2,0},{3,1},{4,6},{5,7},{6,4},{7,5},{8,10},{9,11},{10,... | collective-permute-start | bytes 3145736 | tf_op jit(solution)/shard_map/ppermute | solution.py:379
  174.4 56.6 %collective-permute-start.8 = (bf16[2,1024,256]{2,1,0:T(8,128)(2,1)}, bf16[2,1024,256]{2,1,0:T(8,128)(2,1)}, u32[]{:S(2)}, u32[]{:S(2)}) collective-permute-start(bf16[2,1024,256]{2,1,0:T(8,128)(2,1)} %collective-permute-done.refs_4_), channel_id=1, source_target_pairs={{0,1},{1,0},{2,3},{3,2},{4,5},{5,4},{6,7},{7,6},{8,9},{9,8},{10,11... | collective-permute-start | bytes 3145736 | tf_op jit(solution)/shard_map/ppermute | solution.py:379
  180.7 51.5 %collective-permute-start.10 = (bf16[2,1024,256]{2,1,0:T(8,128)(2,1)}, bf16[2,1024,256]{2,1,0:T(8,128)(2,1)}, u32[]{:S(2)}, u32[]{:S(2)}) collective-permute-start(bf16[2,1024,256]{2,1,0:T(8,128)(2,1)} %collective-permute-done.3.refs_8_), channel_id=1, source_target_pairs={{0,16},{16,0},{1,17},{17,1},{2,18},{18,2},{3,19},{19,3},{4,20},{20... | collective-permute-start | bytes 3145736 | tf_op jit(solution)/shard_map/ppermute | solution.py:384
  181.9 50.6 %collective-permute-start.11 = (bf16[2,1024,256]{2,1,0:T(8,128)(2,1)}, bf16[2,1024,256]{2,1,0:T(8,128)(2,1)}, u32[]{:S(2)}, u32[]{:S(2)}) collective-permute-start(bf16[2,1024,256]{2,1,0:T(8,128)(2,1)} %collective-permute-done.3.refs_8_), channel_id=1, source_target_pairs={{0,1},{1,0},{2,3},{3,2},{4,5},{5,4},{6,7},{7,6},{8,9},{9,8},{10,11... | collective-permute-start | bytes 3145736 | tf_op jit(solution)/shard_map/ppermute | solution.py:379
  182.2 50.5 %collective-permute-start.13 = (bf16[2,1024,256]{2,1,0:T(8,128)(2,1)}, bf16[2,1024,256]{2,1,0:T(8,128)(2,1)}, u32[]{:S(2)}, u32[]{:S(2)}) collective-permute-start(bf16[2,1024,256]{2,1,0:T(8,128)(2,1)} %collective-permute-done.4.refs_12_), channel_id=1, source_target_pairs={{0,16},{16,0},{1,17},{17,1},{2,18},{18,2},{3,19},{19,3},{4,20},{20... | collective-permute-start | bytes 3145736 | tf_op jit(solution)/shard_map/ppermute | solution.py:384
  214.2 18.9 %collective-permute-start.14 = (bf16[2,1024,256]{2,1,0:T(8,128)(2,1)}, bf16[2,1024,256]{2,1,0:T(8,128)(2,1)}, u32[]{:S(2)}, u32[]{:S(2)}) collective-permute-start(bf16[2,1024,256]{2,1,0:T(8,128)(2,1)} %collective-permute-done.4.refs_12_), channel_id=1, source_target_pairs={{0,1},{1,0},{2,3},{3,2},{4,5},{5,4},{6,7},{7,6},{8,9},{9,8},{10,11... | collective-permute-start | bytes 3145736 | tf_op jit(solution)/shard_map/ppermute | solution.py:379
  225.4 5.5 %copy-start.5 = (s32[16]{0:T(128)}, s32[16]{0:T(128)S(1)}, u32[]{:S(2)}) copy-start(s32[16]{0:T(128)S(1)} %stack.89.src_ref) | copy-start | bytes 196
  230.9 69.6 %collective-permute-start.18 = (bf16[2,1024,256]{2,1,0:T(8,128)(2,1)}, bf16[2,1024,256]{2,1,0:T(8,128)(2,1)}, u32[]{:S(2)}, u32[]{:S(2)}) collective-permute-start(bf16[2,1024,256]{2,1,0:T(8,128)(2,1)} %collective-permute-done.16.refs_16_), channel_id=1, source_target_pairs={{0,16},{16,0},{1,17},{17,1},{2,18},{18,2},{3,19},{19,3},{4,20},{20... | collective-permute-start | bytes 3145736 | tf_op jit(solution)/shard_map/ppermute | solution.py:384
  232.2 68.7 %collective-permute-start.19 = (bf16[2,1024,256]{2,1,0:T(8,128)(2,1)}, bf16[2,1024,256]{2,1,0:T(8,128)(2,1)}, u32[]{:S(2)}, u32[]{:S(2)}) collective-permute-start(bf16[2,1024,256]{2,1,0:T(8,128)(2,1)} %collective-permute-done.16.refs_16_), channel_id=1, source_target_pairs={{0,1},{1,0},{2,3},{3,2},{4,5},{5,4},{6,7},{7,6},{8,9},{9,8},{10,11... | collective-permute-start | bytes 3145736 | tf_op jit(solution)/shard_map/ppermute | solution.py:379
  232.5 65.3 %collective-permute-start.9 = (bf16[2,1024,256]{2,1,0:T(8,128)(2,1)}, bf16[2,1024,256]{2,1,0:T(8,128)(2,1)}, u32[]{:S(2)}, u32[]{:S(2)}) collective-permute-start(bf16[2,1024,256]{2,1,0:T(8,128)(2,1)} %collective-permute-done.7.refs_5_), channel_id=1, source_target_pairs={{0,1},{1,0},{2,3},{3,2},{4,5},{5,4},{6,7},{7,6},{8,9},{9,8},{10,11... | collective-permute-start | bytes 3145736 | tf_op jit(solution)/shard_map/ppermute | solution.py:379
  232.8 65.3 %collective-permute-start.12 = (bf16[2,1024,256]{2,1,0:T(8,128)(2,1)}, bf16[2,1024,256]{2,1,0:T(8,128)(2,1)}, u32[]{:S(2)}, u32[]{:S(2)}) collective-permute-start(bf16[2,1024,256]{2,1,0:T(8,128)(2,1)} %collective-permute-done.10.refs_9_), channel_id=1, source_target_pairs={{0,1},{1,0},{2,3},{3,2},{4,5},{5,4},{6,7},{7,6},{8,9},{9,8},{10,11... | collective-permute-start | bytes 3145736 | tf_op jit(solution)/shard_map/ppermute | solution.py:379
  233.0 66.1 %collective-permute-start.15 = (bf16[2,1024,256]{2,1,0:T(8,128)(2,1)}, bf16[2,1024,256]{2,1,0:T(8,128)(2,1)}, u32[]{:S(2)}, u32[]{:S(2)}) collective-permute-start(bf16[2,1024,256]{2,1,0:T(8,128)(2,1)} %collective-permute-done.13.refs_13_), channel_id=1, source_target_pairs={{0,1},{1,0},{2,3},{3,2},{4,5},{5,4},{6,7},{7,6},{8,9},{9,8},{10,11... | collective-permute-start | bytes 3145736 | tf_op jit(solution)/shard_map/ppermute | solution.py:379
  233.3 4.2 copy-start
  274.7 23.0 %all-to-all-start = ((f32[16,3,10,128]{3,1,2,0:T(4,128)}), f32[16,3,10,128]{3,1,2,0:T(4,128)S(1)}, u32[]{:S(2)}, u32[]{:S(2)}) async-start(f32[16,3,10,128]{3,1,2,0:T(4,128)} %copy.89), calls=%async_computation | async-start | bytes 655360 | tf_op jit(solution)/shard_map/all_to_all | solution.py:437
  297.9 24.1 %collective-permute-start.21 = (bf16[2,1024,256]{2,1,0:T(8,128)(2,1)}, bf16[2,1024,256]{2,1,0:T(8,128)(2,1)S(1)}, u32[]{:S(2)}, u32[]{:S(2)}) collective-permute-start(bf16[2,1024,256]{2,1,0:T(8,128)(2,1)} %collective-permute-done.17.refs_20_), channel_id=1, source_target_pairs={{0,16},{16,0},{1,17},{17,1},{2,18},{18,2},{3,19},{19,3},{4,20},{20... | collective-permute-start | bytes 3145736 | tf_op jit(solution)/shard_map/ppermute | solution.py:384
  298.0 27.0 %collective-permute-start.22 = (bf16[2,1024,256]{2,1,0:T(8,128)(2,1)}, bf16[2,1024,256]{2,1,0:T(8,128)(2,1)}, u32[]{:S(2)}, u32[]{:S(2)}) collective-permute-start(bf16[2,1024,256]{2,1,0:T(8,128)(2,1)} %collective-permute-done.17.refs_20_), channel_id=1, source_target_pairs={{0,1},{1,0},{2,3},{3,2},{4,5},{5,4},{6,7},{7,6},{8,9},{9,8},{10,11... | collective-permute-start | bytes 3145736 | tf_op jit(solution)/shard_map/ppermute | solution.py:379
  299.1 45.5 %collective-permute-start.24 = (bf16[2,1024,256]{2,1,0:T(8,128)(2,1)}, bf16[2,1024,256]{2,1,0:T(8,128)(2,1)}, u32[]{:S(2)}, u32[]{:S(2)}) collective-permute-start(bf16[2,1024,256]{2,1,0:T(8,128)(2,1)} %collective-permute-done.1.refs_24_), channel_id=1, source_target_pairs={{0,16},{16,0},{1,17},{17,1},{2,18},{18,2},{3,19},{19,3},{4,20},{20... | collective-permute-start | bytes 3145736 | tf_op jit(solution)/shard_map/ppermute | solution.py:384
  300.6 47.1 %collective-permute-start.25 = (bf16[2,1024,256]{2,1,0:T(8,128)(2,1)}, bf16[2,1024,256]{2,1,0:T(8,128)(2,1)}, u32[]{:S(2)}, u32[]{:S(2)}) collective-permute-start(bf16[2,1024,256]{2,1,0:T(8,128)(2,1)} %collective-permute-done.1.refs_24_), channel_id=1, source_target_pairs={{0,1},{1,0},{2,3},{3,2},{4,5},{5,4},{6,7},{7,6},{8,9},{9,8},{10,11... | collective-permute-start | bytes 3145736 | tf_op jit(solution)/shard_map/ppermute | solution.py:379
  300.9 66.2 %collective-permute-start.27 = (bf16[2,1024,256]{2,1,0:T(8,128)(2,1)}, bf16[2,1024,256]{2,1,0:T(8,128)(2,1)}, u32[]{:S(2)}, u32[]{:S(2)}) collective-permute-start(bf16[2,1024,256]{2,1,0:T(8,128)(2,1)} %collective-permute-done.2.refs_28_), channel_id=1, source_target_pairs={{0,16},{16,0},{1,17},{17,1},{2,18},{18,2},{3,19},{19,3},{4,20},{20... | collective-permute-start | bytes 3145736 | tf_op jit(solution)/shard_map/ppermute | solution.py:384
  322.0 52.8 %copy-start.6 = (bf16[2,1024,256]{2,1,0:T(8,128)(2,1)}, bf16[2,1024,256]{2,1,0:T(8,128)(2,1)S(1)}, u32[]{:S(2)}) copy-start(bf16[2,1024,256]{2,1,0:T(8,128)(2,1)S(1)} %collective-permute-done.21.refs_21_) | copy-start | bytes 3145732
  322.0 55.4 %collective-permute-start.28 = (bf16[2,1024,256]{2,1,0:T(8,128)(2,1)}, bf16[2,1024,256]{2,1,0:T(8,128)(2,1)}, u32[]{:S(2)}, u32[]{:S(2)}) collective-permute-start(bf16[2,1024,256]{2,1,0:T(8,128)(2,1)} %collective-permute-done.2.refs_28_), channel_id=1, source_target_pairs={{0,1},{1,0},{2,3},{3,2},{4,5},{5,4},{6,7},{7,6},{8,9},{9,8},{10,11... | collective-permute-start | bytes 3145736 | tf_op jit(solution)/shard_map/ppermute | solution.py:379
  325.0 52.4 %collective-permute-start.20 = (bf16[2,1024,256]{2,1,0:T(8,128)(2,1)}, bf16[2,1024,256]{2,1,0:T(8,128)(2,1)}, u32[]{:S(2)}, u32[]{:S(2)}) collective-permute-start(bf16[2,1024,256]{2,1,0:T(8,128)(2,1)} %collective-permute-done.18.refs_17_), channel_id=1, source_target_pairs={{0,1},{1,0},{2,3},{3,2},{4,5},{5,4},{6,7},{7,6},{8,9},{9,8},{10,11... | collective-permute-start | bytes 3145736 | tf_op jit(solution)/shard_map/ppermute | solution.py:379
  344.6 32.8 %collective-permute-start.23 = (bf16[2,1024,256]{2,1,0:T(8,128)(2,1)S(1)}, bf16[2,1024,256]{2,1,0:T(8,128)(2,1)}, u32[]{:S(2)}, u32[]{:S(2)}) collective-permute-start(bf16[2,1024,256]{2,1,0:T(8,128)(2,1)S(1)} %collective-permute-done.21.refs_21_), channel_id=1, source_target_pairs={{0,1},{1,0},{2,3},{3,2},{4,5},{5,4},{6,7},{7,6},{8,9},{9,8},{10,11... | collective-permute-start | bytes 3145736 | tf_op jit(solution)/shard_map/ppermute | solution.py:379
  347.6 29.8 %collective-permute-start.26 = (bf16[2,1024,256]{2,1,0:T(8,128)(2,1)}, bf16[2,1024,256]{2,1,0:T(8,128)(2,1)}, u32[]{:S(2)}, u32[]{:S(2)}) collective-permute-start(bf16[2,1024,256]{2,1,0:T(8,128)(2,1)} %collective-permute-done.24.refs_25_), channel_id=1, source_target_pairs={{0,1},{1,0},{2,3},{3,2},{4,5},{5,4},{6,7},{7,6},{8,9},{9,8},{10,11... | collective-permute-start | bytes 3145736 | tf_op jit(solution)/shard_map/ppermute | solution.py:379
  367.1 10.4 %collective-permute-start.29 = (bf16[2,1024,256]{2,1,0:T(8,128)(2,1)}, bf16[2,1024,256]{2,1,0:T(8,128)(2,1)}, u32[]{:S(2)}, u32[]{:S(2)}) collective-permute-start(bf16[2,1024,256]{2,1,0:T(8,128)(2,1)} %collective-permute-done.27.refs_29_), channel_id=1, source_target_pairs={{0,1},{1,0},{2,3},{3,2},{4,5},{5,4},{6,7},{7,6},{8,9},{9,8},{10,11... | collective-permute-start | bytes 3145736 | tf_op jit(solution)/shard_map/ppermute | solution.py:379
Sparse Core Ops, SparseCore 0:
  108.5 200.3 all-gather.1
